TPU v7x, 32 devices: a whole 2x2x4 slice. The times are simulated.
32 devices in a mesh: groups: 2 (over y), tp: 4 (over x, core), dp: 4 (over z).
Axes of the slice: x: 2, y: 2, z: 4, core: 2. Of those that a mesh axis runs over, the one named last changes fastest.
Arguments:
- hidden: bfloat16 [128, 2560], P(('groups', 'dp'), 'tp'), parts along dimension 0, may hold values from -40 to 40
- in_gain: float32 [2560], replicated, may hold values from 0.1 to 1.9
- z_weight: bfloat16 [2560, 5120], P(None, 'tp'), may hold values from -0.125 to 0.125
- x_weight: bfloat16 [2560, 5120], P(None, 'tp'), may hold values from -0.125 to 0.125
- bc_weight: bfloat16 [2560, 256], P(None, 'tp'), may hold values from -0.125 to 0.125
- dt_weight: bfloat16 [2560, 80], P(None, 'tp'), may hold values from -0.125 to 0.125
- conv_x_weight: bfloat16 [4, 5120], P(None, 'tp'), may hold values from -3 to 3
- conv_x_bias: bfloat16 [5120], P('tp'), may hold values from -3 to 3
- conv_bc_weight: bfloat16 [4, 256], P(None, 'tp'), may hold values from -3 to 3
- conv_bc_bias: bfloat16 [256], P('tp'), may hold values from -3 to 3
- conv_x_state: bfloat16 [128, 3, 5120], P(('groups', 'dp'), None, 'tp'), parts along dimension 0, may hold values from -6 to 6
- conv_bc_state: bfloat16 [128, 3, 256], P(('groups', 'dp'), None, 'tp'), parts along dimension 0, may hold values from -6 to 6
- dt_bias: float32 [80], P('tp'), may hold values from -4 to -1
- log_rate: float32 [80], P('tp'), may hold values from 0 to 2.5
- skip_gain: float32 [80], P('tp'), may hold values from 0.5 to 2
- ssm_state: float32 [128, 80, 64, 128], P(('groups', 'dp'), 'tp'), parts along dimension 0, may hold values from -20 to 20
- norm_gain: float32 [5120], P('tp'), may hold values from 0.1 to 1.9
- out_weight: bfloat16 [5120, 2560], P('tp'), may hold values from -0.125 to 0.125
- pool_slot: int32 [8, 16], P(('groups', 'dp')), parts along dimension 0, may hold values from 0 to 15, as said below
- active: int32 [128], P(('groups', 'dp')), parts along dimension 0, may hold values 0 or 1
Outputs:
- layer_out: bfloat16 [128, 2560], P(('groups', 'dp'), 'tp'), parts along dimension 0
- conv_x_next: bfloat16 [128, 3, 5120], P(('groups', 'dp'), None, 'tp'), parts along dimension 0
- conv_bc_next: bfloat16 [128, 3, 256], P(('groups', 'dp'), None, 'tp'), parts along dimension 0
- ssm_next: float32 [128, 80, 64, 128], P(('groups', 'dp'), 'tp'), parts along dimension 0
There are 2 independent parts, one for each index of `groups`. A program takes and returns all parts, laid end to end along the dimension named above; an argument that names none is the same for every part. Nothing has to cross between parts.
Inputs may be any that keep to these rules, and one draw needn't show every extreme that they name: `pool_slot`: each row is a permutation of 0 to 15.
All inputs are finite; a program needn't handle non-finite values. No bound on the sum of `active` on one device may be relied on, other than what follows from the above.
Results may differ from a plain program's by a relative error of at most 0.0085.
Values may be sent and summed in bfloat16 or wider, within the bound.
A program may use at most 128 MiB of HBM per device.

v0:
```python
import functools

import jax
import jax.numpy as jnp
from jax import lax
from jax.experimental import pallas as pl
from jax.experimental.pallas import tpu as pltpu
from jax.sharding import PartitionSpec as P

F32 = jnp.float32
BF16 = jnp.bfloat16
VMEM = pl.BlockSpec(memory_space=pltpu.VMEM)
SMEM = pl.BlockSpec(memory_space=pltpu.SMEM)
ANY = pl.BlockSpec(memory_space=pl.ANY)
HBM = pl.BlockSpec(memory_space=pltpu.HBM)
NT = (((1,), (1,)), ((), ()))
TN = (((0,), (0,)), ((), ()))


def silu(v):
    return v / (1.0 + jnp.exp(-v))


def softplus(v):
    return jnp.maximum(v, 0.0) + jnp.log1p(jnp.exp(-jnp.abs(v)))


def slot_matrix(slot_row):
    rows = slot_row.shape[1]
    return slot_row == lax.broadcasted_iota(jnp.int32, (rows, rows), 0)


def greet(n):
    me = lax.axis_index("tp")
    barrier = pltpu.get_barrier_semaphore()
    for off in range(1, n):
        pl.semaphore_signal(
            barrier,
            inc=1,
            device_id={"tp": lax.rem(me + off, n)},
            device_id_type=pl.DeviceIdType.MESH,
        )
    pl.semaphore_wait(barrier, n - 1)


def push(src, dst, send, recv, off, n):
    copy = pltpu.make_async_remote_copy(
        src_ref=src,
        dst_ref=dst,
        send_sem=send.at[off],
        recv_sem=recv.at[off],
        device_id={"tp": lax.rem(lax.axis_index("tp") + off, n)},
        device_id_type=pl.DeviceIdType.MESH,
    )
    copy.start()
    return copy


def project_kernel(
    n,
    hidden, gain_h, zw, xw, bcw_h, dtw_h, bc_taps_h, bc_bias_h, bc_state_h, dt_bias_h, log_rate_h,
    slot_h, active_h, state_h,
    z_out, x_out, bcp_out, bc_out, dt_out, decay_out, state_out,
    hid_all, feed, zbuf, xbuf, bc_send, bc_all,
    gain, bcw, dtw, bc_taps, bc_bias, bc_state, dt_bias, log_rate, slot, active,
    zsem, xsem, hs, hr, bs, br, own_sem, small_sem, state_sem,
):
    me = lax.axis_index("tp")
    seqs, feats = hidden.shape
    own = pltpu.make_async_copy(hidden, hid_all.at[me], own_sem)
    own.start()
    smalls = []
    pairs = (
        (slot_h, slot), (active_h, active), (gain_h, gain), (bcw_h, bcw), (dtw_h, dtw),
        (bc_taps_h, bc_taps), (bc_bias_h, bc_bias), (bc_state_h, bc_state),
        (dt_bias_h, dt_bias), (log_rate_h, log_rate),
    )
    for k, (src, dst) in enumerate(pairs):
        copy = pltpu.make_async_copy(src, dst, small_sem.at[k])
        copy.start()
        smalls.append(copy)
    blocks = [lax.rem(me + n - off, n) for off in range(n)]
    loads = []
    for off, block in enumerate(blocks):
        rows = pl.ds(pl.multiple_of(block * feats, feats), feats)
        xc = pltpu.make_async_copy(xw.at[rows, :], xbuf.at[off], xsem.at[off])
        zc = pltpu.make_async_copy(zw.at[rows, :], zbuf.at[off], zsem.at[off])
        xc.start()
        zc.start()
        loads.append((xc, zc))
    state_copy = pltpu.make_async_copy(state_h, state_out, state_sem)
    state_copy.start()
    greet(n)
    own.wait()
    sends = [push(hid_all.at[me], hid_all.at[me], hs, hr, off, n) for off in range(1, n)]
    for copy in smalls:
        copy.wait()
    onehot = slot_matrix(slot[...])
    perm = onehot.astype(F32).astype(BF16)
    live = jnp.sum(jnp.where(onehot, active[...], 0), axis=1, keepdims=True) > 0
    gains = gain[...].reshape(1, -1)
    gains = [gains[:, j * feats : (j + 1) * feats] for j in range(n)]
    own_gain = gains[0]
    for j in range(1, n):
        own_gain = jnp.where(me == j, gains[j], own_gain)

    def fed(block, block_gain):
        return jnp.dot(
            perm, (block.astype(F32) * block_gain).astype(BF16), preferred_element_type=F32
        ).astype(BF16)

    part = fed(hid_all[me], own_gain)
    loads[0][0].wait()
    x = jnp.dot(part, xbuf[0], preferred_element_type=F32)
    loads[0][1].wait()
    z = jnp.dot(part, zbuf[0], preferred_element_type=F32)

    for copy in sends:
        copy.wait()
    squares = jnp.zeros((seqs, 1), F32)
    for j in range(n):
        block = hid_all[j]
        feed[j] = fed(block, gains[j])
        wide = block.astype(F32)
        squares += jnp.sum(wide * wide, axis=1, keepdims=True)
    inv = lax.rsqrt(squares / (n * feats) + 1e-05)
    inv = jnp.dot(
        onehot.astype(F32), jnp.broadcast_to(inv, (seqs, 128)),
        precision=lax.Precision.HIGHEST, preferred_element_type=F32,
    )[:, :1]
    whole = jnp.concatenate([feed[j] for j in range(n)], axis=1)
    bcp = lax.dot_general(whole, bcw[...], NT, preferred_element_type=F32)
    bcp = (bcp * inv).astype(BF16)
    bcp_out[...] = bcp
    acc = bcp.astype(F32) * bc_taps[3:4, :].astype(F32)
    for t in range(3):
        acc += bc_state[t].astype(F32) * bc_taps[t : t + 1, :].astype(F32)
    bc_send[...] = silu(acc + bc_bias[...].astype(F32).reshape(1, -1)).astype(BF16)
    bc_all[me] = bc_send[...]
    dtp = lax.dot_general(whole, dtw[...], NT, preferred_element_type=F32)
    sends = [push(bc_send, bc_all.at[me], bs, br, off, n) for off in range(1, n)]
    dt = softplus((dtp * inv).astype(BF16).astype(F32) + dt_bias[...].reshape(1, -1))
    dt_out[...] = dt
    decay_out[...] = jnp.where(live, jnp.exp(-dt * jnp.exp(log_rate[...].reshape(1, -1))), 1.0)

    for off in range(1, n):
        part = feed[blocks[off]]
        loads[off][0].wait()
        x += jnp.dot(part, xbuf[off], preferred_element_type=F32)
        loads[off][1].wait()
        z += jnp.dot(part, zbuf[off], preferred_element_type=F32)
    z_out[...] = (z * inv).astype(BF16)
    x_out[...] = (x * inv).astype(BF16)
    for copy in sends:
        copy.wait()
    bc_out[...] = jnp.concatenate([bc_all[j] for j in range(n)], axis=1)
    state_copy.wait()


def state_kernel(
    n, group,
    decay, decay_v, dt, z_proj, x_proj, bcp, bc, x_taps, x_bias, x_state, bc_state, skip, norm_gain,
    slot, active, state, out_w,
    x_next, bc_next, state_next, branch, sq,
    st, ow, ut, yb, c_rows, osem, wsem,
):
    seqs, heads, hp, ns = st.shape
    chans = heads * hp
    wcopy = pltpu.make_async_copy(out_w, ow, wsem)
    wcopy.start()

    onehot = slot_matrix(slot[...])
    live = jnp.sum(jnp.where(onehot, active[...], 0), axis=1, keepdims=True) > 0
    x_new = x_proj[...]
    acc = x_new.astype(F32) * x_taps[3:4, :].astype(F32)
    for t in range(3):
        acc += x_state[t].astype(F32) * x_taps[t : t + 1, :].astype(F32)
    xc = silu(acc + x_bias[...].astype(F32).reshape(1, -1)).astype(BF16).astype(F32)
    for old, new, nxt in ((x_state, x_new, x_next), (bc_state, bcp[...], bc_next)):
        nxt[0] = jnp.where(live, old[1], old[0])
        nxt[1] = jnp.where(live, old[2], old[1])
        nxt[2] = jnp.where(live, new, old[2])

    spread = (
        lax.broadcasted_iota(jnp.int32, (heads, chans), 1) // hp
        == lax.broadcasted_iota(jnp.int32, (heads, chans), 0)
    ).astype(F32)
    dt_wide = jnp.dot(dt[...], spread, precision=lax.Precision.HIGHEST, preferred_element_type=F32)
    skip_wide = jnp.dot(
        skip[...], spread, precision=lax.Precision.HIGHEST, preferred_element_type=F32
    )
    decay_wide = jnp.dot(
        decay_v[...], spread, precision=lax.Precision.HIGHEST, preferred_element_type=F32
    )
    u = jnp.where(live, dt_wide * xc, 0.0)
    high = u.astype(BF16).astype(F32)
    ut[...] = jnp.concatenate([high, u - high], axis=0).T.astype(BF16)
    b_rows = bc[:, :ns].astype(F32)
    b_twice = jnp.concatenate([b_rows, b_rows], axis=0)
    row_id = lax.broadcasted_iota(jnp.int32, (2 * seqs, ns), 0)
    c_rows[...] = bc[:, ns:].astype(F32)
    along = jnp.sum(b_rows * c_rows[...], axis=1, keepdims=True)

    def step(b, carry):
        b_one = jnp.where((row_id == b) | (row_id == b + seqs), b_twice, 0.0).astype(BF16)
        c_one = c_rows[pl.ds(b, 1), :].astype(BF16)
        for g in range(heads // group):
            lo = g * group * hp
            width = group * hp
            outer = jnp.dot(ut[lo : lo + width, :], b_one, preferred_element_type=F32)
            heads_here = pl.ds(g * group, group)
            old = state[b, heads_here].reshape(width, ns).astype(BF16)
            yb[pl.ds(b, 1), lo : lo + width] = lax.dot_general(
                c_one, old, NT, preferred_element_type=F32
            )
            for k in range(group):
                h = g * group + k
                st[b, h] = decay[b, h] * state[b, h] + outer[k * hp : (k + 1) * hp, :]
        pltpu.make_async_copy(st.at[b], state_next.at[b], osem.at[b]).start()
        return carry

    lax.fori_loop(0, seqs, step, 0, unroll=4)

    y = decay_wide * yb[...] + u * along + skip_wide * xc
    gated = y * silu(z_proj[...].astype(F32))
    perm = onehot.astype(F32)
    sq_slot = jnp.sum(gated * gated, axis=1, keepdims=True)
    sq_row = jnp.sum(perm * sq_slot, axis=0, keepdims=True)
    eye = lax.broadcasted_iota(jnp.int32, (seqs, seqs), 0) == lax.broadcasted_iota(
        jnp.int32, (seqs, seqs), 1
    )
    sq_col = jnp.sum(jnp.where(eye, sq_row, 0.0), axis=1, keepdims=True)
    sq[...] = jnp.broadcast_to(sq_col, sq.shape)
    scaled = (gated * norm_gain[...].reshape(1, -1)).astype(BF16)
    scaled = lax.dot_general(
        perm.astype(BF16), scaled, TN, preferred_element_type=F32
    ).astype(BF16)
    wcopy.wait()
    width = branch.shape[2]
    for j in range(n):
        branch[j] = jnp.dot(
            scaled, ow[:, j * width : (j + 1) * width], preferred_element_type=F32
        ).astype(BF16)

    def drain(b, carry):
        pltpu.make_async_copy(st.at[b], state_next.at[b], osem.at[b]).wait()
        return carry

    lax.fori_loop(0, seqs, drain, 0)


def reduce_kernel(n, inner, branch, sq, hidden, active, out, parts, sqs, ps, pr, qs, qr):
    me = lax.axis_index("tp")
    greet(n)
    copies = []
    for off in range(1, n):
        peer = lax.rem(me + off, n)
        copies.append(push(branch.at[peer], parts.at[off], ps, pr, off, n))
        copies.append(push(sq, sqs.at[off], qs, qr, off, n))
    rows = hidden.shape[0]
    eye = lax.broadcasted_iota(jnp.int32, (rows, rows), 0) == lax.broadcasted_iota(
        jnp.int32, (rows, rows), 1
    )
    live = jnp.sum(jnp.where(eye, active[...], 0), axis=1, keepdims=True) > 0
    old = hidden[...]
    total = branch[me].astype(F32)
    squares = sq[:, :1]
    for copy in copies:
        copy.wait()
    for off in range(1, n):
        total += parts[off].astype(F32)
        squares += sqs[off][:, :1]
    inv = lax.rsqrt(squares / inner + 1e-05)
    out[...] = jnp.where(live, (old.astype(F32) + inv * total).astype(BF16), old)


def shards(
    n,
    hidden, in_gain, z_weight, x_weight, bc_weight, dt_weight,
    conv_x_weight, conv_x_bias, conv_bc_weight, conv_bc_bias, conv_x_state, conv_bc_state,
    dt_bias, log_rate, skip_gain, ssm_state, norm_gain, out_weight, pool_slot, active,
):
    seqs, feats = hidden.shape
    model, chans = z_weight.shape
    bc_own = bc_weight.shape[1]
    heads, hp, ns = ssm_state.shape[1:]
    in_hbm = lambda v: pltpu.with_memory_space_constraint(v, pltpu.HBM)
    row = lambda v: v.reshape(1, -1)
    active = row(active)
    x_old = jnp.transpose(conv_x_state, (1, 0, 2))
    bc_old = jnp.transpose(conv_bc_state, (1, 0, 2))
    dma = pltpu.SemaphoreType.DMA
    shape = jax.ShapeDtypeStruct
    z, x, bcp, bc, dt, decay, held = pl.pallas_call(
        functools.partial(project_kernel, n),
        out_shape=(
            shape((seqs, chans), BF16),
            shape((seqs, chans), BF16),
            shape((seqs, bc_own), BF16),
            shape((seqs, bc_own * n), BF16),
            shape((seqs, heads), F32),
            shape((seqs, heads), F32),
            pltpu.VMEM(ssm_state.shape, F32),
        ),
        in_specs=[HBM] * 14,
        out_specs=(VMEM,) * 7,
        scratch_shapes=[
            pltpu.VMEM((n, seqs, feats), BF16),
            pltpu.VMEM((n, seqs, feats), BF16),
            pltpu.VMEM((n, feats, chans), BF16),
            pltpu.VMEM((n, feats, chans), BF16),
            pltpu.VMEM((seqs, bc_own), BF16),
            pltpu.VMEM((n, seqs, bc_own), BF16),
            pltpu.VMEM(in_gain.shape, F32),
            pltpu.VMEM((bc_own, model), BF16),
            pltpu.VMEM((heads, model), BF16),
            pltpu.VMEM(conv_bc_weight.shape, BF16),
            pltpu.VMEM(conv_bc_bias.shape, BF16),
            pltpu.VMEM(bc_old.shape, BF16),
            pltpu.VMEM(dt_bias.shape, F32),
            pltpu.VMEM(log_rate.shape, F32),
            pltpu.VMEM(pool_slot.shape, jnp.int32),
            pltpu.VMEM(active.shape, jnp.int32),
            dma((n,)), dma((n,)), dma((n,)), dma((n,)), dma((n,)), dma((n,)), dma(()), dma((10,)), dma(()),
        ],
        compiler_params=pltpu.CompilerParams(collective_id=0, has_side_effects=True, vmem_limit_bytes=20 * 2**20),
        name="project",
    )(*map(in_hbm, (
        hidden, in_gain, z_weight, x_weight, bc_weight.T, dt_weight.T,
        conv_bc_weight, conv_bc_bias, bc_old, dt_bias, log_rate, pool_slot, active, ssm_state,
    )))
    x_next, bc_next, state_next, branch, sq = pl.pallas_call(
        functools.partial(state_kernel, n, 4 if heads % 4 == 0 else heads),
        out_shape=(
            shape(x_old.shape, BF16),
            shape(bc_old.shape, BF16),
            shape(ssm_state.shape, F32),
            shape((n, seqs, feats), BF16),
            shape((seqs, 128), F32),
        ),
        in_specs=[SMEM] + [VMEM] * 15 + [HBM],
        out_specs=(VMEM, VMEM, HBM, VMEM, VMEM),
        scratch_shapes=[
            pltpu.VMEM(ssm_state.shape, F32),
            pltpu.VMEM(out_weight.shape, BF16),
            pltpu.VMEM((chans, 2 * seqs), BF16),
            pltpu.VMEM((seqs, chans), F32),
            pltpu.VMEM((seqs, ns), F32),
            dma((seqs,)), dma(()),
        ],
        compiler_params=pltpu.CompilerParams(vmem_limit_bytes=20 * 2**20),
        name="state",
    )(
        decay, decay, dt, z, x, bcp, bc, conv_x_weight, conv_x_bias, x_old, bc_old,
        row(skip_gain), norm_gain, pool_slot, active, held, in_hbm(out_weight),
    )
    layer_out = pl.pallas_call(
        functools.partial(reduce_kernel, n, chans * n),
        out_shape=shape((seqs, feats), BF16),
        in_specs=[VMEM] * 4,
        out_specs=VMEM,
        scratch_shapes=[
            pltpu.VMEM((n, seqs, feats), BF16),
            pltpu.VMEM((n, seqs, 128), F32),
            dma((n,)), dma((n,)), dma((n,)), dma((n,)),
        ],
        compiler_params=pltpu.CompilerParams(collective_id=1, has_side_effects=True, vmem_limit_bytes=2 * 2**20),
        name="reduce",
    )(branch, sq, hidden, active)
    return (
        layer_out,
        jnp.transpose(x_next, (1, 0, 2)),
        jnp.transpose(bc_next, (1, 0, 2)),
        state_next,
    )


def solution(mesh):
    rows = ("groups", "dp")
    placed = (
        P(rows, "tp"), P(), P(None, "tp"), P(None, "tp"), P(None, "tp"), P(None, "tp"),
        P(None, "tp"), P("tp"), P(None, "tp"), P("tp"),
        P(rows, None, "tp"), P(rows, None, "tp"),
        P("tp"), P("tp"), P("tp"), P(rows, "tp", None, None), P("tp"), P("tp", None),
        P(rows, None), P(rows),
    )
    return jax.shard_map(
        functools.partial(shards, mesh.shape["tp"]),
        mesh=mesh,
        in_specs=placed,
        out_specs=(
            P(rows, "tp"), P(rows, None, "tp"), P(rows, None, "tp"), P(rows, "tp", None, None),
        ),
        check_vma=False,
    )
```

profile of v0, /device:TPU:0, one launch (start us, length us, event | category | flops | bytes accessed | tf_op | source)
XLA Modules:
  0.0 25.9 jit_solution(6473652619995194059)
XLA Ops:
  0.6 0.0 copy-start
  0.6 0.0 copy-start.2
  0.7 0.0 copy-start.3
  0.7 0.0 copy-start.4
  0.7 0.0 copy-start.5
  0.7 0.0 copy-start.6
  0.7 0.0 copy-start.7
  0.7 0.0 copy-start.8
  0.7 10.9 %project.1 = (bf16[16,1280]{1,0:T(8,128)(2,1)S(1)}, bf16[16,1280]{1,0:T(8,128)(2,1)S(1)}, bf16[16,64]{1,0:T(8,128)(2,1)S(1)}, bf16[16,256]{1,0:T(8,128)(2,1)S(1)...) custom-call(bf16[16,640]{1,0:T(8,128)(2,1)} %hidden.3, f32[2560]{0:T(1024)} %gain_h.1, ...), custom_call_target="tpu_custom_call" | custom-call | tf_op jit(solution)/shard_map/project/pallas_call | solution.py:294
  11.6 0.0 copy-start.1
  11.6 0.0 copy-done
  11.6 0.0 copy-done.2
  11.6 0.0 copy-done.3
  11.6 0.0 copy-done.4
  11.6 0.0 copy-done.5
  11.7 0.0 copy-done.6
  11.7 0.0 copy-done.7
  11.7 0.0 copy-done.8
  11.7 9.3 %state.1 = (bf16[3,16,1280]{2,1,0:T(8,128)(2,1)}, bf16[3,16,64]{2,1,0:T(8,128)(2,1)}, f32[16,20,64,128]{3,2,1,0:T(8,128)}, bf16[4,16,640]{2,1,0:T(8,128)(2,1)S(1)}, f32[16,128]{1,0:T(8,128)S(1)}) custom-call(f32[16,20]{1,0:T(8,128)S(1)} %get-tuple-element.16.decay.decay_v, f32[16,20]{1,0:T(8,128)S(1)} %get-tuple-element.16.decay.decay_v, ...), custom_call_target="tpu_custom_call" | custom-call | tf_op jit(solution)/shard_map/state/pallas_call | solution.py:332
  21.0 0.0 copy-done.1
  21.0 4.2 %reduce.1 = bf16[16,640]{1,0:T(8,128)(2,1)S(1)} custom-call(bf16[4,16,640]{2,1,0:T(8,128)(2,1)S(1)} %get-tuple-element.23.branch, f32[16,128]{1,0:T(8,128)S(1)} %get-tuple-element.24.sq, bf16[16,640]{1,0:T(8,128)(2,1)S(1)} %copy-done.1, s32[1,16]{1,0:T(1,128)S(1)} %bitcast.13), custom_call_target="tpu_custom_call" | custom-call | tf_op jit(solution)/shard_map/reduce/pallas_call | solution.py:357
  25.2 0.6 %copy.25 = bf16[16,640]{1,0:T(8,128)(2,1)} copy(bf16[16,640]{1,0:T(8,128)(2,1)S(1)} %reduce.1) | data formatting | bytes 40960
Async XLA Ops:
  0.6 11.0 %copy-start = (bf16[16,3,1280]{2,0,1:T(8,128)(2,1)S(1)}, bf16[16,3,1280]{2,0,1:T(8,128)(2,1)}, u32[]{:S(2)}) copy-start(bf16[16,3,1280]{2,0,1:T(8,128)(2,1)} %param.30) | copy-start | bytes 368644
  0.6 11.0 %copy-start.2 = (bf16[16,3,64]{2,0,1:T(8,128)(2,1)S(1)}, bf16[16,3,64]{2,0,1:T(8,128)(2,1)}, u32[]{:S(2)}) copy-start(bf16[16,3,64]{2,0,1:T(8,128)(2,1)} %param.31) | copy-start | bytes 18436
  0.7 11.0 %copy-start.3 = (bf16[4,1280]{1,0:T(4,128)(2,1)S(1)}, bf16[4,1280]{1,0:T(4,128)(2,1)}, u32[]{:S(2)}) copy-start(bf16[4,1280]{1,0:T(4,128)(2,1)} %x_taps.1) | copy-start | bytes 30724
  0.7 11.0 %copy-start.4 = (f32[1280]{0:T(1024)S(1)}, f32[1280]{0:T(1024)}, u32[]{:S(2)}) copy-start(f32[1280]{0:T(1024)} %norm_gain.1) | copy-start | bytes 15364
  0.7 11.0 %copy-start.5 = (s32[16]{0:T(128)S(1)}, s32[16]{0:T(128)}, u32[]{:S(2)}) copy-start(s32[16]{0:T(128)} %param.39) | copy-start | bytes 196
  0.7 11.0 %copy-start.6 = (bf16[1280]{0:T(1024)(128)(2,1)S(1)}, bf16[1280]{0:T(1024)(128)(2,1)}, u32[]{:S(2)}) copy-start(bf16[1280]{0:T(1024)(128)(2,1)} %x_bias.1) | copy-start | bytes 7684
  0.7 11.0 %copy-start.7 = (s32[1,16]{1,0:T(1,128)S(1)}, s32[1,16]{1,0:T(1,128)}, u32[]{:S(2)}) copy-start(s32[1,16]{1,0:T(1,128)} %slot.1) | copy-start | bytes 196
  0.7 11.0 %copy-start.8 = (f32[20]{0:T(128)S(1)}, f32[20]{0:T(128)}, u32[]{:S(2)}) copy-start(f32[20]{0:T(128)} %param.34) | copy-start | bytes 244
  11.6 9.4 %copy-start.1 = (bf16[16,640]{1,0:T(8,128)(2,1)S(1)}, bf16[16,640]{1,0:T(8,128)(2,1)}, u32[]{:S(2)}) copy-start(bf16[16,640]{1,0:T(8,128)(2,1)} %hidden.3) | copy-start | bytes 61444
where the time goes:
time: 26 us; the launch traced here: 25.9 us
  Pallas kernels  24.4 us (94%)
  between operations  0.81 us (3%)
  local copies, waits for them, and re-layouts  0.65 us (2%)
    pallas_call x1, Pallas kernels, shards(): pl.pallas_call(functools.partial(project_kernel, n), out_shape=(shape((se...  10.9 us
    pallas_call x1, Pallas kernels, shards(): pl.pallas_call(functools.partial(state_kernel, n, 4 if heads % 4 == 0 els...  9.33 us
    pallas_call x1, Pallas kernels, shards(): pl.pallas_call(functools.partial(reduce_kernel, n, chans * n), out_shape=...  4.21 us
    unnamed x19, local copies, waits for them, and re-layouts  0.65 us

commit v1 on v0

--- a/solution.py
+++ b/solution.py
@@ -15,6 +15,8 @@
 HBM = pl.BlockSpec(memory_space=pltpu.HBM)
 NT = (((1,), (1,)), ((), ()))
 TN = (((0,), (0,)), ((), ()))
+STEPS = 4
+ROWS = 256
 
 
 def silu(v):
@@ -274,7 +276,410 @@
     out[...] = jnp.where(live, (old.astype(F32) + inv * total).astype(BF16), old)
 
 
-def shards(
+def flip(v, k):
+    bit = 1
+    while bit <= k:
+        if k & bit:
+            v = v + (1 - 2 * lax.rem(v // bit, 2)) * bit
+        bit *= 2
+    return v
+
+
+def swap(src, dst, send, recv, k):
+    return pltpu.make_async_remote_copy(
+        src_ref=src,
+        dst_ref=dst,
+        send_sem=send.at[k],
+        recv_sem=recv.at[k],
+        device_id={"tp": flip(lax.axis_index("tp"), k)},
+        device_id_type=pl.DeviceIdType.MESH,
+    )
+
+
+def front_kernel(
+    n, steps,
+    hidden, gain_h, zw, xw, bcw_h, dtw_h, ow_h, x_taps_h, x_bias_h, x_state_h,
+    bc_taps_h, bc_bias_h, bc_state_h, dt_bias_h, log_rate_h, skip_h, norm_gain_h, slot_h, active_h, state_h,
+    x_out, bcp_out, ut_out, b_out, dec_out, total_out, sq_out, state_out,
+    own, hid, zbuf, xbuf, bcwbuf, dtwbuf, owbuf, bc_send, bc_all, yt, part_send, parts, sq_send, sqs,
+    gain, x_taps, x_bias, x_state, bc_taps, bc_bias, bc_state, dt_bias, log_rate, skip, norm_gain, slot, active,
+    own_sem, small_sem, xsem, zsem, bcsem, dtsem, ssem, wsem, hs, hr, bs, br, ps, pr, qs, qr,
+):
+    me = lax.axis_index("tp")
+    seqs, feats = hidden.shape
+    chans = x_out.shape[1]
+    heads = dec_out.shape[0]
+    ns = state_h.shape[3]
+    hp = chans // heads
+    far = list(range(2, n)) + list(range(1, min(n, 2)))
+    blocks = [flip(me, k) for k in range(n)]
+    spans = [pl.ds(pl.multiple_of(b * feats, feats), feats) for b in blocks]
+
+    own_copy = pltpu.make_async_copy(hidden, own, own_sem)
+    own_copy.start()
+    pairs = (
+        (slot_h, slot), (active_h, active), (gain_h, gain),
+        (bc_taps_h, bc_taps), (bc_bias_h, bc_bias), (bc_state_h, bc_state),
+        (dt_bias_h, dt_bias), (log_rate_h, log_rate), (skip_h, skip),
+        (x_taps_h, x_taps), (x_bias_h, x_bias), (x_state_h, x_state), (norm_gain_h, norm_gain),
+    )
+    smalls = [pltpu.make_async_copy(s, d, small_sem.at[i]) for i, (s, d) in enumerate(pairs)]
+    for copy in smalls:
+        copy.start()
+    xc = [pltpu.make_async_copy(xw.at[spans[k], :], xbuf.at[k], xsem.at[k]) for k in range(n)]
+    zc = [pltpu.make_async_copy(zw.at[spans[k], :], zbuf.at[k], zsem.at[k]) for k in range(n)]
+    bcc = [pltpu.make_async_copy(bcw_h.at[:, spans[k]], bcwbuf.at[k], bcsem.at[k]) for k in range(n)]
+    dtc = [pltpu.make_async_copy(dtw_h.at[:, spans[k]], dtwbuf.at[k], dtsem.at[k]) for k in range(n)]
+    owc = [pltpu.make_async_copy(ow_h.at[:, spans[k]], owbuf.at[k], wsem.at[k]) for k in range(n)]
+    span = seqs // steps
+    stc = [
+        pltpu.make_async_copy(
+            state_h.at[pl.ds(q * span, span)], state_out.at[pl.ds(q * span, span)], ssem.at[q]
+        )
+        for q in range(steps)
+    ]
+    order = [xc[0], zc[0]] + bcc + dtc
+    for k in range(1, n):
+        order += [xc[k], zc[k]]
+    order += stc + [owc[k] for k in far] + [owc[0]]
+    for copy in order:
+        copy.start(priority=1)
+
+    barrier = pltpu.get_barrier_semaphore()
+    for k in range(1, n):
+        pl.semaphore_signal(
+            barrier, inc=1, device_id={"tp": blocks[k]}, device_id_type=pl.DeviceIdType.MESH
+        )
+    own_copy.wait()
+    smalls[0].wait()
+    onehot = slot_matrix(slot[...])
+    perm = onehot.astype(F32).astype(BF16)
+    hid[0] = jnp.dot(perm, own[...], preferred_element_type=F32).astype(BF16)
+    pl.semaphore_wait(barrier, n - 1)
+    hid_swaps = {k: swap(hid.at[0], hid.at[k], hs, hr, k) for k in far}
+    for k in far:
+        hid_swaps[k].start()
+
+    for copy in smalls[1:]:
+        copy.wait()
+    live = jnp.sum(jnp.where(onehot, active[...], 0), axis=1, keepdims=True) > 0
+    gains = gain[...].reshape(1, -1)
+    gains = [gains[:, j * feats : (j + 1) * feats] for j in range(n)]
+
+    def fed(k):
+        block_gain = gains[0]
+        for j in range(1, n):
+            block_gain = jnp.where(blocks[k] == j, gains[j], block_gain)
+        return (hid[k].astype(F32) * block_gain).astype(BF16)
+
+    def squared(k):
+        wide = hid[k].astype(F32)
+        return jnp.sum(wide * wide, axis=1, keepdims=True)
+
+    def narrow(k, part):
+        bcc[k].wait()
+        dtc[k].wait()
+        return (
+            lax.dot_general(part, bcwbuf[k], NT, preferred_element_type=F32),
+            lax.dot_general(part, dtwbuf[k], NT, preferred_element_type=F32),
+        )
+
+    feed = fed(0)
+    squares = squared(0)
+    xc[0].wait()
+    x = jnp.dot(feed, xbuf[0], preferred_element_type=F32)
+    zc[0].wait()
+    z = jnp.dot(feed, zbuf[0], preferred_element_type=F32)
+    bcp, dtp = narrow(0, feed)
+    feeds = {}
+    for k in [1] + far[:-1]:
+        hid_swaps[k].wait_recv()
+        feeds[k] = fed(k)
+        squares += squared(k)
+        more = narrow(k, feeds[k])
+        bcp += more[0]
+        dtp += more[1]
+        if k == 1:
+            xc[1].wait()
+            x += jnp.dot(feeds[1], xbuf[1], preferred_element_type=F32)
+            zc[1].wait()
+            z += jnp.dot(feeds[1], zbuf[1], preferred_element_type=F32)
+    inv = lax.rsqrt(squares / (n * feats) + 1e-05)
+    bcp = (bcp * inv).astype(BF16)
+    bcp_out[...] = bcp
+    acc = bcp.astype(F32) * bc_taps[3:4, :].astype(F32)
+    for t in range(3):
+        acc += bc_state[t].astype(F32) * bc_taps[t : t + 1, :].astype(F32)
+    bc_send[...] = silu(acc + bc_bias[...].astype(F32).reshape(1, -1)).astype(BF16)
+    bc_all[me] = bc_send[...]
+    bc_swaps = {k: swap(bc_send, bc_all.at[me], bs, br, k) for k in far}
+    for k in far:
+        bc_swaps[k].start()
+
+    for k in far[:-1]:
+        xc[k].wait()
+        x += jnp.dot(feeds[k], xbuf[k], preferred_element_type=F32)
+        zc[k].wait()
+        z += jnp.dot(feeds[k], zbuf[k], preferred_element_type=F32)
+    dt = softplus((dtp * inv).astype(BF16).astype(F32) + dt_bias[...].reshape(1, -1))
+    decay = jnp.where(live, jnp.exp(-dt * jnp.exp(log_rate[...].reshape(1, -1))), 1.0)
+    for h in range(heads):
+        dec_out[h] = jnp.broadcast_to(decay[:, h : h + 1], (seqs, ns))
+    spread = (
+        lax.broadcasted_iota(jnp.int32, (heads, chans), 1) // hp
+        == lax.broadcasted_iota(jnp.int32, (heads, chans), 0)
+    ).astype(F32).astype(BF16)
+    per_head = jnp.concatenate(
+        [dt, decay, jnp.broadcast_to(skip[...].reshape(1, -1), (8, heads))], axis=0
+    )
+    high = per_head.astype(BF16)
+    rest = per_head - high.astype(F32)
+    mid = rest.astype(BF16)
+    low = (rest - mid.astype(F32)).astype(BF16)
+    wide = sum(jnp.dot(v, spread, preferred_element_type=F32) for v in (high, mid, low))
+    dt_wide, decay_wide, skip_wide = wide[:seqs], wide[seqs : 2 * seqs], wide[2 * seqs : 2 * seqs + 1]
+
+    x_new = (x * inv).astype(BF16)
+    x_out[...] = x_new
+    acc = x_new.astype(F32) * x_taps[3:4, :].astype(F32)
+    for t in range(3):
+        acc += x_state[t].astype(F32) * x_taps[t : t + 1, :].astype(F32)
+    conv = silu(acc + x_bias[...].astype(F32).reshape(1, -1)).astype(BF16).astype(F32)
+    u = jnp.where(live, dt_wide * conv, 0.0)
+    high = u.astype(BF16).astype(F32)
+    ut_out[...] = jnp.concatenate([high, u - high], axis=0).T.astype(BF16)
+    gate = silu((z * inv).astype(BF16).astype(F32))
+
+    for k in far:
+        bc_swaps[k].wait_recv()
+    both = jnp.concatenate([bc_all[j] for j in range(n)], axis=1).astype(F32)
+    b_rows = both[:, :ns]
+    c_rows = both[:, ns:]
+    b_out[...] = b_rows
+    along = jnp.sum(b_rows * c_rows, axis=1, keepdims=True)
+    row_id = lax.broadcasted_iota(jnp.int32, (seqs, ns), 0)
+    tile = ROWS if chans % ROWS == 0 else chans
+    for q in range(steps):
+        stationary = jnp.concatenate(
+            [jnp.where(row_id == q * span + i, c_rows, 0.0).astype(BF16) for i in range(span)], axis=1
+        )
+        stationary = jnp.concatenate(
+            [stationary, jnp.zeros((128 - seqs, span * ns), BF16)], axis=0
+        )
+        stc[q].wait()
+        for lo in range(0, chans, tile):
+            moving = jnp.concatenate(
+                [
+                    state_out[q * span + i, lo // hp : (lo + tile) // hp].reshape(tile, ns).astype(BF16)
+                    for i in range(span)
+                ],
+                axis=1,
+            )
+            got = lax.dot_general(moving, stationary, NT, preferred_element_type=F32)
+            if q:
+                yt[lo : lo + tile, :] += got
+            else:
+                yt[lo : lo + tile, :] = got
+    old_y = yt[...].T[:seqs]
+    y = decay_wide * old_y + u * along + skip_wide * conv
+    gated = y * gate
+    sq_own = jnp.broadcast_to(jnp.sum(gated * gated, axis=1, keepdims=True), sq_send.shape)
+    sq_send[...] = sq_own
+    scaled = (gated * norm_gain[...].reshape(1, -1)).astype(BF16)
+    tails = []
+    for i, k in enumerate(far):
+        owc[k].wait()
+        part_send[k] = jnp.dot(scaled, owbuf[k], preferred_element_type=F32).astype(BF16)
+        if i == 0:
+            for j in far:
+                tails.append(swap(sq_send, sqs.at[j], qs, qr, j))
+                tails[-1].start()
+        tails.append(swap(part_send.at[k], parts.at[k], ps, pr, k))
+        tails[-1].start()
+    owc[0].wait()
+    total = jnp.dot(scaled, owbuf[0], preferred_element_type=F32)
+    for copies in (hid_swaps, bc_swaps):
+        for k in far:
+            copies[k].wait_send()
+    for copy in tails:
+        copy.wait()
+    for k in far:
+        total += parts[k].astype(F32)
+        sq_own += sqs[k]
+    total_out[...] = total
+    sq_out[...] = sq_own
+
+
+def back_kernel(
+    inner,
+    hidden, slot, active, total, sq, x_new, x_state, bcp, bc_state, ut, b_rows, dec, state,
+    layer_h, x_next_h, bc_next_h, state_next,
+    layer, x_next, bc_next, st, osem, lsem,
+):
+    seqs, heads, hp, ns = st.shape
+    row_id = lax.broadcasted_iota(jnp.int32, (2 * seqs, ns), 0)
+    b_twice = jnp.concatenate([b_rows[...], b_rows[...]], axis=0)
+    pack = 128 // hp
+
+    def write(p):
+        both = pl.ds(2 * p, 2)
+        return pltpu.make_async_copy(st.at[both], state_next.at[both], osem.at[p])
+
+    def step(p, carry):
+        stationary = jnp.concatenate(
+            [
+                jnp.where((row_id == 2 * p + i) | (row_id == 2 * p + i + seqs), b_twice, 0.0).astype(BF16)
+                for i in range(2)
+            ],
+            axis=1,
+        )
+        for lo in range(0, heads, pack):
+            outer = jnp.dot(ut[lo * hp : (lo + pack) * hp, :], stationary, preferred_element_type=F32)
+            for i in range(2):
+                for h in range(pack):
+                    st[2 * p + i, lo + h] = (
+                        dec[lo + h, pl.ds(2 * p + i, 1), :] * state[2 * p + i, lo + h]
+                        + outer[h * hp : (h + 1) * hp, i * ns : (i + 1) * ns]
+                    )
+        write(p).start()
+        return carry
+
+    step(0, 0)
+    onehot = slot_matrix(slot[...])
+    live = jnp.sum(jnp.where(onehot, active[...], 0), axis=1, keepdims=True) > 0
+    for old, new, nxt in ((x_state, x_new[...], x_next), (bc_state, bcp[...], bc_next)):
+        nxt[0] = jnp.where(live, old[1], old[0])
+        nxt[1] = jnp.where(live, old[2], old[1])
+        nxt[2] = jnp.where(live, new, old[2])
+    eye = lax.broadcasted_iota(jnp.int32, (seqs, seqs), 0) == lax.broadcasted_iota(
+        jnp.int32, (seqs, seqs), 1
+    )
+    live = jnp.sum(jnp.where(eye, active[...], 0), axis=1, keepdims=True) > 0
+    inv = lax.rsqrt(sq[:, :1] / inner + 1e-05)
+    delta = lax.dot_general(
+        onehot.astype(F32), inv * total[...], TN,
+        precision=lax.Precision.HIGHEST, preferred_element_type=F32,
+    )
+    old = hidden[...]
+    layer[...] = jnp.where(live, (old.astype(F32) + delta).astype(BF16), old)
+    outs = [
+        pltpu.make_async_copy(s, d, lsem.at[i])
+        for i, (s, d) in enumerate(((layer, layer_h), (x_next, x_next_h), (bc_next, bc_next_h)))
+    ]
+    for copy in outs:
+        copy.start()
+    lax.fori_loop(1, seqs // 2, step, 0)
+    for copy in outs:
+        copy.wait()
+
+    def drain(p, carry):
+        write(p).wait()
+        return carry
+
+    lax.fori_loop(0, seqs // 2, drain, 0)
+
+
+def shards(n, *args):
+    hidden, z_weight, ssm_state = args[0], args[2], args[15]
+    seqs, feats = hidden.shape
+    chans = z_weight.shape[1]
+    heads, hp, ns = ssm_state.shape[1:]
+    aligned = feats % 128 == 0 and chans % 128 == 0 and ns == 128 and 128 % hp == 0
+    if aligned and n > 1 and n & (n - 1) == 0 and seqs % 16 == 0 and seqs <= 128:
+        return fast_shards(n, *args)
+    return plain_shards(n, *args)
+
+
+def fast_shards(
+    n,
+    hidden, in_gain, z_weight, x_weight, bc_weight, dt_weight,
+    conv_x_weight, conv_x_bias, conv_bc_weight, conv_bc_bias, conv_x_state, conv_bc_state,
+    dt_bias, log_rate, skip_gain, ssm_state, norm_gain, out_weight, pool_slot, active,
+):
+    seqs, feats = hidden.shape
+    model, chans = z_weight.shape
+    bc_own = bc_weight.shape[1]
+    heads, hp, ns = ssm_state.shape[1:]
+    steps = STEPS
+    in_hbm = lambda v: pltpu.with_memory_space_constraint(v, pltpu.HBM)
+    active = active.reshape(1, -1)
+    x_old = jnp.transpose(conv_x_state, (1, 0, 2))
+    bc_old = jnp.transpose(conv_bc_state, (1, 0, 2))
+    dma = pltpu.SemaphoreType.DMA
+    shape = jax.ShapeDtypeStruct
+    like = lambda v: pltpu.VMEM(v.shape, v.dtype)
+    x_new, bcp, ut, b_rows, dec, total, sq, held = pl.pallas_call(
+        functools.partial(front_kernel, n, steps),
+        out_shape=(
+            shape((seqs, chans), BF16),
+            shape((seqs, bc_own), BF16),
+            shape((chans, 2 * seqs), BF16),
+            shape((seqs, ns), F32),
+            shape((heads, seqs, ns), F32),
+            shape((seqs, feats), F32),
+            shape((seqs, 128), F32),
+            pltpu.VMEM(ssm_state.shape, F32),
+        ),
+        in_specs=[HBM] * 20,
+        out_specs=(VMEM,) * 8,
+        scratch_shapes=[
+            like(hidden),
+            pltpu.VMEM((n, seqs, feats), BF16),
+            pltpu.VMEM((n, feats, chans), BF16),
+            pltpu.VMEM((n, feats, chans), BF16),
+            pltpu.VMEM((n, bc_own, feats), BF16),
+            pltpu.VMEM((n, heads, feats), BF16),
+            pltpu.VMEM((n, chans, feats), BF16),
+            pltpu.VMEM((seqs, bc_own), BF16),
+            pltpu.VMEM((n, seqs, bc_own), BF16),
+            pltpu.VMEM((chans, 128), F32),
+            pltpu.VMEM((n, seqs, feats), BF16),
+            pltpu.VMEM((n, seqs, feats), BF16),
+            pltpu.VMEM((seqs, 128), F32),
+            pltpu.VMEM((n, seqs, 128), F32),
+            like(in_gain), like(conv_x_weight), like(conv_x_bias), like(x_old),
+            like(conv_bc_weight), like(conv_bc_bias), like(bc_old),
+            like(dt_bias), like(log_rate), like(skip_gain), like(norm_gain), like(pool_slot), like(active),
+            dma(()), dma((13,)), dma((n,)), dma((n,)), dma((n,)), dma((n,)), dma((steps,)), dma((n,)),
+            dma((n,)), dma((n,)), dma((n,)), dma((n,)), dma((n,)), dma((n,)), dma((n,)), dma((n,)),
+        ],
+        compiler_params=pltpu.CompilerParams(
+            collective_id=0, has_side_effects=True, vmem_limit_bytes=28 * 2**20
+        ),
+        name="front",
+    )(*map(in_hbm, (
+        hidden, in_gain, z_weight, x_weight, bc_weight.T, dt_weight.T, out_weight,
+        conv_x_weight, conv_x_bias, x_old, conv_bc_weight, conv_bc_bias, bc_old,
+        dt_bias, log_rate, skip_gain, norm_gain, pool_slot, active, ssm_state,
+    )))
+    layer_out, x_next, bc_next, state_next = pl.pallas_call(
+        functools.partial(back_kernel, chans * n),
+        out_shape=(
+            shape(hidden.shape, BF16),
+            shape(x_old.shape, BF16),
+            shape(bc_old.shape, BF16),
+            shape(ssm_state.shape, F32),
+        ),
+        in_specs=[VMEM] * 13,
+        out_specs=(HBM,) * 4,
+        scratch_shapes=[
+            like(hidden), like(x_old), like(bc_old), like(ssm_state),
+            dma((seqs // 2,)), dma((3,)),
+        ],
+        compiler_params=pltpu.CompilerParams(vmem_limit_bytes=16 * 2**20),
+        name="back",
+    )(
+        hidden, pool_slot, active, total, sq, x_new, x_old, bcp, bc_old, ut, b_rows, dec, held,
+    )
+    return (
+        layer_out,
+        jnp.transpose(x_next, (1, 0, 2)),
+        jnp.transpose(bc_next, (1, 0, 2)),
+        state_next,
+    )
+
+
+def plain_shards(
     n,
     hidden, in_gain, z_weight, x_weight, bc_weight, dt_weight,
     conv_x_weight, conv_x_bias, conv_bc_weight, conv_bc_bias, conv_x_state, conv_bc_state,

time: 26 us -> 23.2 us (0.89)
  Pallas kernels: 24.4 us -> 22.3 us
  local copies, waits for them, and re-layouts: 0.65 us -> 0.02 us
    pallas_call x3 -> x2, Pallas kernels: 24.4 us -> 22.3 us  [the longest x1 17.9 us: fast_shards(): pl.pallas_call(functools.partial(front_kernel, n, steps), out_shape=(shap...]
    unnamed x19 -> x10, local copies, waits for them, and re-layouts: 0.65 us -> 0.02 us
where the time goes in v1:
time: 23.2 us; the launch traced here: 23.1 us
  Pallas kernels  22.3 us (96%)
  between operations  0.73 us (3%)
    pallas_call x1, Pallas kernels, fast_shards(): pl.pallas_call(functools.partial(front_kernel, n, steps), out_shape=(shap...  17.9 us
    pallas_call x1, Pallas kernels, fast_shards(): pl.pallas_call(functools.partial(back_kernel, chans * n), out_shape=(shap...  4.45 us

profile of v1, /device:TPU:0, one launch (start us, length us, event | category | flops | bytes accessed | tf_op | source)
XLA Modules:
  0.0 23.1 jit_solution(6548062605867428526)
XLA Ops:
  0.6 0.0 copy-start
  0.6 0.0 copy-start.1
  0.7 0.0 copy-start.2
  0.7 0.0 copy-start.3
  0.7 0.0 copy-start.4
  0.7 17.9 %front.1 = (bf16[16,1280]{1,0:T(8,128)(2,1)S(1)}, bf16[16,64]{1,0:T(8,128)(2,1)S(1)}, bf16[1280,32]{1,0:T(8,128)(2,1)S(1)}, f32[16,128]{1,0:T(8,128)S(1)}, f32[2...) custom-call(bf16[16,640]{1,0:T(8,128)(2,1)} %hidden.3, ...), custom_call_target="tpu_custom_call" | custom-call | tf_op jit(solution)/shard_map/front/pallas_call | solution.py:611
  18.6 0.0 copy-done
  18.6 0.0 copy-done.1
  18.6 0.0 copy-done.2
  18.6 0.0 copy-done.3
  18.6 0.0 copy-done.4
  18.6 4.5 %back.1 = (bf16[16,640]{1,0:T(8,128)(2,1)}, bf16[3,16,1280]{2,1,0:T(8,128)(2,1)}, bf16[3,16,64]{2,1,0:T(8,128)(2,1)}, f32[16,20,64,128]{3,2,1,0:T(8,128)}) custom-call(bf16[16,640]{1,0:T(8,128)(2,1)S(1)} %copy-done.1, s32[1,16]{1,0:T(1,128)S(1)} %copy-done.3, s32[1,16]{1,0:T(1,128)S(1)} %bitcast.12, f32[16,640]{1,0:T(8,128)S(1)} %get-tuple-element.16.total, ...), custom_call_target="tpu_custom_call" | custom-call | tf_op jit(solution)/shard_map/back/pallas_call | solution.py:655
Async XLA Ops:
  0.6 17.9 %copy-start = (bf16[16,3,1280]{2,0,1:T(8,128)(2,1)S(1)}, bf16[16,3,1280]{2,0,1:T(8,128)(2,1)}, u32[]{:S(2)}) copy-start(bf16[16,3,1280]{2,0,1:T(8,128)(2,1)} %param.30) | copy-start | bytes 368644
  0.6 17.9 %copy-start.1 = (bf16[16,640]{1,0:T(8,128)(2,1)S(1)}, bf16[16,640]{1,0:T(8,128)(2,1)}, u32[]{:S(2)}) copy-start(bf16[16,640]{1,0:T(8,128)(2,1)} %hidden.3) | copy-start | bytes 61444
  0.7 17.9 %copy-start.2 = (bf16[16,3,64]{2,0,1:T(8,128)(2,1)S(1)}, bf16[16,3,64]{2,0,1:T(8,128)(2,1)}, u32[]{:S(2)}) copy-start(bf16[16,3,64]{2,0,1:T(8,128)(2,1)} %param.31) | copy-start | bytes 18436
  0.7 17.9 %copy-start.3 = (s32[1,16]{1,0:T(1,128)S(1)}, s32[1,16]{1,0:T(1,128)}, u32[]{:S(2)}) copy-start(s32[1,16]{1,0:T(1,128)} %slot.1) | copy-start | bytes 196
  0.7 17.9 %copy-start.4 = (s32[16]{0:T(128)S(1)}, s32[16]{0:T(128)}, u32[]{:S(2)}) copy-start(s32[16]{0:T(128)} %param.39) | copy-start | bytes 196

commit v2 on v1

--- a/solution.py
+++ b/solution.py
@@ -300,10 +300,10 @@
     n, steps,
     hidden, gain_h, zw, xw, bcw_h, dtw_h, ow_h, x_taps_h, x_bias_h, x_state_h,
     bc_taps_h, bc_bias_h, bc_state_h, dt_bias_h, log_rate_h, skip_h, norm_gain_h, slot_h, active_h, state_h,
-    x_out, bcp_out, ut_out, b_out, dec_out, total_out, sq_out, state_out,
-    own, hid, zbuf, xbuf, bcwbuf, dtwbuf, owbuf, bc_send, bc_all, yt, part_send, parts, sq_send, sqs,
+    x_out, bcp_out, ut_out, b_out, dec_out, mine_out, sq_send, parts, sqs, state_out,
+    own, hid, zbuf, xbuf, bcw, dtw, owbuf, bc_send, bc_all, yt, part_send,
     gain, x_taps, x_bias, x_state, bc_taps, bc_bias, bc_state, dt_bias, log_rate, skip, norm_gain, slot, active,
-    own_sem, small_sem, xsem, zsem, bcsem, dtsem, ssem, wsem, hs, hr, bs, br, ps, pr, qs, qr,
+    own_sem, small_sem, xsem, zsem, ssem, wsem, hs, hr, bs, br, ps, pr, qs, qr,
 ):
     me = lax.axis_index("tp")
     seqs, feats = hidden.shape
@@ -320,7 +320,7 @@
     pairs = (
         (slot_h, slot), (active_h, active), (gain_h, gain),
         (bc_taps_h, bc_taps), (bc_bias_h, bc_bias), (bc_state_h, bc_state),
-        (dt_bias_h, dt_bias), (log_rate_h, log_rate), (skip_h, skip),
+        (dt_bias_h, dt_bias), (log_rate_h, log_rate), (skip_h, skip), (bcw_h, bcw), (dtw_h, dtw),
         (x_taps_h, x_taps), (x_bias_h, x_bias), (x_state_h, x_state), (norm_gain_h, norm_gain),
     )
     smalls = [pltpu.make_async_copy(s, d, small_sem.at[i]) for i, (s, d) in enumerate(pairs)]
@@ -328,8 +328,6 @@
         copy.start()
     xc = [pltpu.make_async_copy(xw.at[spans[k], :], xbuf.at[k], xsem.at[k]) for k in range(n)]
     zc = [pltpu.make_async_copy(zw.at[spans[k], :], zbuf.at[k], zsem.at[k]) for k in range(n)]
-    bcc = [pltpu.make_async_copy(bcw_h.at[:, spans[k]], bcwbuf.at[k], bcsem.at[k]) for k in range(n)]
-    dtc = [pltpu.make_async_copy(dtw_h.at[:, spans[k]], dtwbuf.at[k], dtsem.at[k]) for k in range(n)]
     owc = [pltpu.make_async_copy(ow_h.at[:, spans[k]], owbuf.at[k], wsem.at[k]) for k in range(n)]
     span = seqs // steps
     stc = [
@@ -338,12 +336,13 @@
         )
         for q in range(steps)
     ]
-    order = [xc[0], zc[0]] + bcc + dtc
-    for k in range(1, n):
-        order += [xc[k], zc[k]]
-    order += stc + [owc[k] for k in far] + [owc[0]]
-    for copy in order:
-        copy.start(priority=1)
+
+    def stream(copies):
+        for copy in copies:
+            copy.start(priority=1)
+
+    for k in range(n):
+        stream([xc[k], zc[k]])
 
     barrier = pltpu.get_barrier_semaphore()
     for k in range(1, n):
@@ -377,11 +376,9 @@
         return jnp.sum(wide * wide, axis=1, keepdims=True)
 
     def narrow(k, part):
-        bcc[k].wait()
-        dtc[k].wait()
         return (
-            lax.dot_general(part, bcwbuf[k], NT, preferred_element_type=F32),
-            lax.dot_general(part, dtwbuf[k], NT, preferred_element_type=F32),
+            lax.dot_general(part, bcw[:, spans[k]], NT, preferred_element_type=F32),
+            lax.dot_general(part, dtw[:, spans[k]], NT, preferred_element_type=F32),
         )
 
     feed = fed(0)
@@ -402,6 +399,7 @@
         if k == 1:
             xc[1].wait()
             x += jnp.dot(feeds[1], xbuf[1], preferred_element_type=F32)
+            stream(stc[: steps // 2])
             zc[1].wait()
             z += jnp.dot(feeds[1], zbuf[1], preferred_element_type=F32)
     inv = lax.rsqrt(squares / (n * feats) + 1e-05)
@@ -415,12 +413,14 @@
     bc_swaps = {k: swap(bc_send, bc_all.at[me], bs, br, k) for k in far}
     for k in far:
         bc_swaps[k].start()
+    stream(stc[steps // 2 :])
 
     for k in far[:-1]:
         xc[k].wait()
         x += jnp.dot(feeds[k], xbuf[k], preferred_element_type=F32)
         zc[k].wait()
         z += jnp.dot(feeds[k], zbuf[k], preferred_element_type=F32)
+    stream([owc[k] for k in far[:2]])
     dt = softplus((dtp * inv).astype(BF16).astype(F32) + dt_bias[...].reshape(1, -1))
     decay = jnp.where(live, jnp.exp(-dt * jnp.exp(log_rate[...].reshape(1, -1))), 1.0)
     for h in range(heads):
@@ -452,6 +452,7 @@
 
     for k in far:
         bc_swaps[k].wait_recv()
+    stream([owc[k] for k in far[2:] + [0]])
     both = jnp.concatenate([bc_all[j] for j in range(n)], axis=1).astype(F32)
     b_rows = both[:, :ns]
     c_rows = both[:, ns:]
@@ -483,8 +484,7 @@
     old_y = yt[...].T[:seqs]
     y = decay_wide * old_y + u * along + skip_wide * conv
     gated = y * gate
-    sq_own = jnp.broadcast_to(jnp.sum(gated * gated, axis=1, keepdims=True), sq_send.shape)
-    sq_send[...] = sq_own
+    sq_send[...] = jnp.broadcast_to(jnp.sum(gated * gated, axis=1, keepdims=True), sq_send.shape)
     scaled = (gated * norm_gain[...].reshape(1, -1)).astype(BF16)
     tails = []
     for i, k in enumerate(far):
@@ -492,27 +492,22 @@
         part_send[k] = jnp.dot(scaled, owbuf[k], preferred_element_type=F32).astype(BF16)
         if i == 0:
             for j in far:
-                tails.append(swap(sq_send, sqs.at[j], qs, qr, j))
+                tails.append(swap(sq_send, sqs.at[j - 1], qs, qr, j))
                 tails[-1].start()
-        tails.append(swap(part_send.at[k], parts.at[k], ps, pr, k))
+        tails.append(swap(part_send.at[k], parts.at[k - 1], ps, pr, k))
         tails[-1].start()
     owc[0].wait()
-    total = jnp.dot(scaled, owbuf[0], preferred_element_type=F32)
+    mine_out[...] = jnp.dot(scaled, owbuf[0], preferred_element_type=F32)
     for copies in (hid_swaps, bc_swaps):
         for k in far:
             copies[k].wait_send()
     for copy in tails:
         copy.wait()
-    for k in far:
-        total += parts[k].astype(F32)
-        sq_own += sqs[k]
-    total_out[...] = total
-    sq_out[...] = sq_own
 
 
 def back_kernel(
     inner,
-    hidden, slot, active, total, sq, x_new, x_state, bcp, bc_state, ut, b_rows, dec, state,
+    hidden, slot, active, mine, sq, parts, sqs, x_new, x_state, bcp, bc_state, ut, b_rows, dec, state,
     layer_h, x_next_h, bc_next_h, state_next,
     layer, x_next, bc_next, st, osem, lsem,
 ):
@@ -555,9 +550,14 @@
         jnp.int32, (seqs, seqs), 1
     )
     live = jnp.sum(jnp.where(eye, active[...], 0), axis=1, keepdims=True) > 0
-    inv = lax.rsqrt(sq[:, :1] / inner + 1e-05)
+    total = mine[...]
+    squares = sq[:, :1]
+    for k in range(parts.shape[0]):
+        total += parts[k].astype(F32)
+        squares += sqs[k][:, :1]
+    inv = lax.rsqrt(squares / inner + 1e-05)
     delta = lax.dot_general(
-        onehot.astype(F32), inv * total[...], TN,
+        onehot.astype(F32), inv * total, TN,
         precision=lax.Precision.HIGHEST, preferred_element_type=F32,
     )
     old = hidden[...]
@@ -608,39 +608,38 @@
     dma = pltpu.SemaphoreType.DMA
     shape = jax.ShapeDtypeStruct
     like = lambda v: pltpu.VMEM(v.shape, v.dtype)
-    x_new, bcp, ut, b_rows, dec, total, sq, held = pl.pallas_call(
+    x_new, bcp, ut, b_rows, dec, mine, sq, parts, sqs, held = pl.pallas_call(
         functools.partial(front_kernel, n, steps),
         out_shape=(
-            shape((seqs, chans), BF16),
-            shape((seqs, bc_own), BF16),
-            shape((chans, 2 * seqs), BF16),
-            shape((seqs, ns), F32),
-            shape((heads, seqs, ns), F32),
-            shape((seqs, feats), F32),
-            shape((seqs, 128), F32),
+            pltpu.VMEM((seqs, chans), BF16),
+            pltpu.VMEM((seqs, bc_own), BF16),
+            pltpu.VMEM((chans, 2 * seqs), BF16),
+            pltpu.VMEM((seqs, ns), F32),
+            pltpu.VMEM((heads, seqs, ns), F32),
+            pltpu.VMEM((seqs, feats), F32),
+            pltpu.VMEM((seqs, 128), F32),
+            pltpu.VMEM((n - 1, seqs, feats), BF16),
+            pltpu.VMEM((n - 1, seqs, 128), F32),
             pltpu.VMEM(ssm_state.shape, F32),
         ),
         in_specs=[HBM] * 20,
-        out_specs=(VMEM,) * 8,
+        out_specs=(VMEM,) * 10,
         scratch_shapes=[
             like(hidden),
             pltpu.VMEM((n, seqs, feats), BF16),
             pltpu.VMEM((n, feats, chans), BF16),
             pltpu.VMEM((n, feats, chans), BF16),
-            pltpu.VMEM((n, bc_own, feats), BF16),
-            pltpu.VMEM((n, heads, feats), BF16),
+            pltpu.VMEM((bc_own, model), BF16),
+            pltpu.VMEM((heads, model), BF16),
             pltpu.VMEM((n, chans, feats), BF16),
             pltpu.VMEM((seqs, bc_own), BF16),
             pltpu.VMEM((n, seqs, bc_own), BF16),
             pltpu.VMEM((chans, 128), F32),
             pltpu.VMEM((n, seqs, feats), BF16),
-            pltpu.VMEM((n, seqs, feats), BF16),
-            pltpu.VMEM((seqs, 128), F32),
-            pltpu.VMEM((n, seqs, 128), F32),
             like(in_gain), like(conv_x_weight), like(conv_x_bias), like(x_old),
             like(conv_bc_weight), like(conv_bc_bias), like(bc_old),
             like(dt_bias), like(log_rate), like(skip_gain), like(norm_gain), like(pool_slot), like(active),
-            dma(()), dma((13,)), dma((n,)), dma((n,)), dma((n,)), dma((n,)), dma((steps,)), dma((n,)),
+            dma(()), dma((15,)), dma((n,)), dma((n,)), dma((steps,)), dma((n,)),
             dma((n,)), dma((n,)), dma((n,)), dma((n,)), dma((n,)), dma((n,)), dma((n,)), dma((n,)),
         ],
         compiler_params=pltpu.CompilerParams(
@@ -660,7 +659,7 @@
             shape(bc_old.shape, BF16),
             shape(ssm_state.shape, F32),
         ),
-        in_specs=[VMEM] * 13,
+        in_specs=[VMEM] * 15,
         out_specs=(HBM,) * 4,
         scratch_shapes=[
             like(hidden), like(x_old), like(bc_old), like(ssm_state),
@@ -669,7 +668,7 @@
         compiler_params=pltpu.CompilerParams(vmem_limit_bytes=16 * 2**20),
         name="back",
     )(
-        hidden, pool_slot, active, total, sq, x_new, x_old, bcp, bc_old, ut, b_rows, dec, held,
+        hidden, pool_slot, active, mine, sq, parts, sqs, x_new, x_old, bcp, bc_old, ut, b_rows, dec, held,
     )
     return (
         layer_out,

time: 23.2 us -> 20.5 us (0.88)
  Pallas kernels: 22.3 us -> 19.6 us
    pallas_call x1, Pallas kernels: 17.9 us -> 15.1 us  [fast_shards(): pl.pallas_call(functools.partial(front_kernel, n, steps), out_shape=(pltp...]
where the time goes in v2:
time: 20.5 us; the launch traced here: 20.3 us
  Pallas kernels  19.6 us (96%)
  between operations  0.73 us (4%)
    pallas_call x1, Pallas kernels, fast_shards(): pl.pallas_call(functools.partial(front_kernel, n, steps), out_shape=(pltp...  15.1 us
    pallas_call x1, Pallas kernels, fast_shards(): pl.pallas_call(functools.partial(back_kernel, chans * n), out_shape=(shap...  4.46 us

profile of v2, /device:TPU:0, one launch (start us, length us, event | category | flops | bytes accessed | tf_op | source)
XLA Modules:
  0.0 20.3 jit_solution(8945584711789320382)
XLA Ops:
  0.6 0.0 copy-start
  0.6 0.0 copy-start.1
  0.7 0.0 copy-start.2
  0.7 0.0 copy-start.3
  0.7 0.0 copy-start.4
  0.7 15.1 %front.1 = (bf16[16,1280]{1,0:T(8,128)(2,1)S(1)}, bf16[16,64]{1,0:T(8,128)(2,1)S(1)}, bf16[1280,32]{1,0:T(8,128)(2,1)S(1)}, f32[16,128]{1,0:T(8,128)S(1)}, f32[2...) custom-call(bf16[16,640]{1,0:T(8,128)(2,1)} %hidden.3, ...), custom_call_target="tpu_custom_call" | custom-call | tf_op jit(solution)/shard_map/front/pallas_call | solution.py:611
  15.8 0.0 copy-done
  15.8 0.0 copy-done.1
  15.8 0.0 copy-done.2
  15.8 0.0 copy-done.3
  15.9 0.0 copy-done.4
  15.9 4.5 %back.1 = (bf16[16,640]{1,0:T(8,128)(2,1)}, bf16[3,16,1280]{2,1,0:T(8,128)(2,1)}, bf16[3,16,64]{2,1,0:T(8,128)(2,1)}, f32[16,20,64,128]{3,2,1,0:T(8,128)}) custom-call(bf16[16,640]{1,0:T(8,128)(2,1)S(1)} %copy-done.1, s32[1,16]{1,0:T(1,128)S(1)} %copy-done.3, s32[1,16]{1,0:T(1,128)S(1)} %bitcast.12, f32[16,640]{1,0:T(8,128)S(1)} %get-tuple-element.18.mine, ...), custom_call_target="tpu_custom_call" | custom-call | tf_op jit(solution)/shard_map/back/pallas_call | solution.py:654
Async XLA Ops:
  0.6 15.2 %copy-start = (bf16[16,3,1280]{2,0,1:T(8,128)(2,1)S(1)}, bf16[16,3,1280]{2,0,1:T(8,128)(2,1)}, u32[]{:S(2)}) copy-start(bf16[16,3,1280]{2,0,1:T(8,128)(2,1)} %param.30) | copy-start | bytes 368644
  0.6 15.2 %copy-start.1 = (bf16[16,640]{1,0:T(8,128)(2,1)S(1)}, bf16[16,640]{1,0:T(8,128)(2,1)}, u32[]{:S(2)}) copy-start(bf16[16,640]{1,0:T(8,128)(2,1)} %hidden.3) | copy-start | bytes 61444
  0.7 15.2 %copy-start.2 = (bf16[16,3,64]{2,0,1:T(8,128)(2,1)S(1)}, bf16[16,3,64]{2,0,1:T(8,128)(2,1)}, u32[]{:S(2)}) copy-start(bf16[16,3,64]{2,0,1:T(8,128)(2,1)} %param.31) | copy-start | bytes 18436
  0.7 15.2 %copy-start.3 = (s32[1,16]{1,0:T(1,128)S(1)}, s32[1,16]{1,0:T(1,128)}, u32[]{:S(2)}) copy-start(s32[1,16]{1,0:T(1,128)} %slot.1) | copy-start | bytes 196
  0.7 15.2 %copy-start.4 = (s32[16]{0:T(128)S(1)}, s32[16]{0:T(128)}, u32[]{:S(2)}) copy-start(s32[16]{0:T(128)} %param.39) | copy-start | bytes 196

commit v3 on v2

--- a/solution.py
+++ b/solution.py
@@ -17,6 +17,7 @@
 TN = (((0,), (0,)), ((), ()))
 STEPS = 4
 ROWS = 256
+READY = 4
 
 
 def silu(v):
@@ -290,20 +291,29 @@
         src_ref=src,
         dst_ref=dst,
         send_sem=send.at[k],
-        recv_sem=recv.at[k],
+        recv_sem=recv.at[k - 1],
         device_id={"tp": flip(lax.axis_index("tp"), k)},
         device_id_type=pl.DeviceIdType.MESH,
     )
 
 
-def front_kernel(
-    n, steps,
+def front_kernel(n, steps, ready, *refs):
+    dma = pltpu.SemaphoreType.DMA
+    pl.run_scoped(
+        functools.partial(front_body, n, steps, ready, *refs),
+        dma(()), dma((15,)), dma((n,)), dma((n,)), dma((steps,)), dma((n,)), dma((n,)), dma((n,)), dma((n,)),
+    )
+
+
+def front_body(
+    n, steps, ready,
     hidden, gain_h, zw, xw, bcw_h, dtw_h, ow_h, x_taps_h, x_bias_h, x_state_h,
     bc_taps_h, bc_bias_h, bc_state_h, dt_bias_h, log_rate_h, skip_h, norm_gain_h, slot_h, active_h, state_h,
-    x_out, bcp_out, ut_out, b_out, dec_out, mine_out, sq_send, parts, sqs, state_out,
+    x_out, bcp_out, ut_out, b_out, dec_out, mine_out, parts, state_out,
     own, hid, zbuf, xbuf, bcw, dtw, owbuf, bc_send, bc_all, yt, part_send,
     gain, x_taps, x_bias, x_state, bc_taps, bc_bias, bc_state, dt_bias, log_rate, skip, norm_gain, slot, active,
-    own_sem, small_sem, xsem, zsem, ssem, wsem, hs, hr, bs, br, ps, pr, qs, qr,
+    hr, br, pr,
+    own_sem, small_sem, xsem, zsem, ssem, wsem, hs, bs, ps,
 ):
     me = lax.axis_index("tp")
     seqs, feats = hidden.shape
@@ -320,11 +330,12 @@
     pairs = (
         (slot_h, slot), (active_h, active), (gain_h, gain),
         (bc_taps_h, bc_taps), (bc_bias_h, bc_bias), (bc_state_h, bc_state),
-        (dt_bias_h, dt_bias), (log_rate_h, log_rate), (skip_h, skip), (bcw_h, bcw), (dtw_h, dtw),
+        (dt_bias_h, dt_bias), (log_rate_h, log_rate), (skip_h, skip),
         (x_taps_h, x_taps), (x_bias_h, x_bias), (x_state_h, x_state), (norm_gain_h, norm_gain),
+        (bcw_h, bcw), (dtw_h, dtw),
     )
     smalls = [pltpu.make_async_copy(s, d, small_sem.at[i]) for i, (s, d) in enumerate(pairs)]
-    for copy in smalls:
+    for copy in smalls[:-2]:
         copy.start()
     xc = [pltpu.make_async_copy(xw.at[spans[k], :], xbuf.at[k], xsem.at[k]) for k in range(n)]
     zc = [pltpu.make_async_copy(zw.at[spans[k], :], zbuf.at[k], zsem.at[k]) for k in range(n)]
@@ -351,6 +362,8 @@
         )
     own_copy.wait()
     smalls[0].wait()
+    for copy in smalls[-2:]:
+        copy.start()
     onehot = slot_matrix(slot[...])
     perm = onehot.astype(F32).astype(BF16)
     hid[0] = jnp.dot(perm, own[...], preferred_element_type=F32).astype(BF16)
@@ -359,7 +372,7 @@
     for k in far:
         hid_swaps[k].start()
 
-    for copy in smalls[1:]:
+    for copy in smalls[1:-2]:
         copy.wait()
     live = jnp.sum(jnp.where(onehot, active[...], 0), axis=1, keepdims=True) > 0
     gains = gain[...].reshape(1, -1)
@@ -387,6 +400,8 @@
     x = jnp.dot(feed, xbuf[0], preferred_element_type=F32)
     zc[0].wait()
     z = jnp.dot(feed, zbuf[0], preferred_element_type=F32)
+    for copy in smalls[-2:]:
+        copy.wait()
     bcp, dtp = narrow(0, feed)
     feeds = {}
     for k in [1] + far[:-1]:
@@ -460,6 +475,7 @@
     along = jnp.sum(b_rows * c_rows, axis=1, keepdims=True)
     row_id = lax.broadcasted_iota(jnp.int32, (seqs, ns), 0)
     tile = ROWS if chans % ROWS == 0 else chans
+    old_y = []
     for q in range(steps):
         stationary = jnp.concatenate(
             [jnp.where(row_id == q * span + i, c_rows, 0.0).astype(BF16) for i in range(span)], axis=1
@@ -477,27 +493,35 @@
                 axis=1,
             )
             got = lax.dot_general(moving, stationary, NT, preferred_element_type=F32)
-            if q:
+            if q == 0:
+                yt[lo : lo + tile, :] = got
+            elif q < steps - 1:
                 yt[lo : lo + tile, :] += got
             else:
-                yt[lo : lo + tile, :] = got
-    old_y = yt[...].T[:seqs]
+                old_y.append((yt[lo : lo + tile, :] + got).T[:seqs])
+    old_y = jnp.concatenate(old_y, axis=1)
     y = decay_wide * old_y + u * along + skip_wide * conv
     gated = y * gate
-    sq_send[...] = jnp.broadcast_to(jnp.sum(gated * gated, axis=1, keepdims=True), sq_send.shape)
+    sq = jnp.sum(gated * gated, axis=1, keepdims=True)
+    high = sq.astype(BF16).astype(F32)
+    mid = (sq - high).astype(BF16).astype(F32)
+    lane = lax.broadcasted_iota(jnp.int32, (seqs, 128), 1)
+    rest = jnp.where(lane == 1, mid, sq - high - mid)
+    coded = jnp.where(lane == 0, high, jnp.where(lane < 3, rest, 0.0))
+    for k in far:
+        part_send[k, :, feats:] = coded.astype(BF16)
+    mine_out[:, feats:] = coded
     scaled = (gated * norm_gain[...].reshape(1, -1)).astype(BF16)
     tails = []
-    for i, k in enumerate(far):
+    for k in far:
         owc[k].wait()
-        part_send[k] = jnp.dot(scaled, owbuf[k], preferred_element_type=F32).astype(BF16)
-        if i == 0:
-            for j in far:
-                tails.append(swap(sq_send, sqs.at[j - 1], qs, qr, j))
-                tails[-1].start()
+        part_send[k, :, :feats] = jnp.dot(scaled, owbuf[k], preferred_element_type=F32).astype(BF16)
         tails.append(swap(part_send.at[k], parts.at[k - 1], ps, pr, k))
         tails[-1].start()
     owc[0].wait()
-    mine_out[...] = jnp.dot(scaled, owbuf[0], preferred_element_type=F32)
+    mine_out[:, :feats] = jnp.dot(scaled, owbuf[0], preferred_element_type=F32)
+    for p in range(ready):
+        update(p, dec_out, ut_out, b_out, state_out, state_out)
     for copies in (hid_swaps, bc_swaps):
         for k in far:
             copies[k].wait_send()
@@ -505,41 +529,49 @@
         copy.wait()
 
 
+def update(p, dec, ut, b_rows, state, out):
+    seqs, heads, hp, ns = state.shape
+    row_id = lax.broadcasted_iota(jnp.int32, (2 * seqs, ns), 0)
+    b_twice = jnp.concatenate([b_rows[...], b_rows[...]], axis=0)
+    stationary = jnp.concatenate(
+        [
+            jnp.where((row_id == 2 * p + i) | (row_id == 2 * p + i + seqs), b_twice, 0.0).astype(BF16)
+            for i in range(2)
+        ],
+        axis=1,
+    )
+    pack = 128 // hp
+    for lo in range(0, heads, pack):
+        outer = jnp.dot(ut[lo * hp : (lo + pack) * hp, :], stationary, preferred_element_type=F32)
+        for i in range(2):
+            for h in range(pack):
+                out[2 * p + i, lo + h] = (
+                    dec[lo + h, pl.ds(2 * p + i, 1), :] * state[2 * p + i, lo + h]
+                    + outer[h * hp : (h + 1) * hp, i * ns : (i + 1) * ns]
+                )
+
+
 def back_kernel(
-    inner,
-    hidden, slot, active, mine, sq, parts, sqs, x_new, x_state, bcp, bc_state, ut, b_rows, dec, state,
+    inner, ready,
+    hidden, slot, active, mine, parts, x_new, x_state, bcp, bc_state, ut, b_rows, dec, state,
     layer_h, x_next_h, bc_next_h, state_next,
     layer, x_next, bc_next, st, osem, lsem,
 ):
-    seqs, heads, hp, ns = st.shape
-    row_id = lax.broadcasted_iota(jnp.int32, (2 * seqs, ns), 0)
-    b_twice = jnp.concatenate([b_rows[...], b_rows[...]], axis=0)
-    pack = 128 // hp
-
-    def write(p):
+    seqs = state.shape[0]
+
+    def write(source, p):
         both = pl.ds(2 * p, 2)
-        return pltpu.make_async_copy(st.at[both], state_next.at[both], osem.at[p])
+        return pltpu.make_async_copy(source.at[both], state_next.at[both], osem.at[p])
+
+    for p in range(ready):
+        write(state, p).start(priority=1)
 
     def step(p, carry):
-        stationary = jnp.concatenate(
-            [
-                jnp.where((row_id == 2 * p + i) | (row_id == 2 * p + i + seqs), b_twice, 0.0).astype(BF16)
-                for i in range(2)
-            ],
-            axis=1,
-        )
-        for lo in range(0, heads, pack):
-            outer = jnp.dot(ut[lo * hp : (lo + pack) * hp, :], stationary, preferred_element_type=F32)
-            for i in range(2):
-                for h in range(pack):
-                    st[2 * p + i, lo + h] = (
-                        dec[lo + h, pl.ds(2 * p + i, 1), :] * state[2 * p + i, lo + h]
-                        + outer[h * hp : (h + 1) * hp, i * ns : (i + 1) * ns]
-                    )
-        write(p).start()
+        update(p, dec, ut, b_rows, state, st)
+        write(st, p).start(priority=1)
         return carry
 
-    step(0, 0)
+    lax.fori_loop(ready, seqs // 2, step, 0)
     onehot = slot_matrix(slot[...])
     live = jnp.sum(jnp.where(onehot, active[...], 0), axis=1, keepdims=True) > 0
     for old, new, nxt in ((x_state, x_new[...], x_next), (bc_state, bcp[...], bc_next)):
@@ -551,11 +583,11 @@
     )
     live = jnp.sum(jnp.where(eye, active[...], 0), axis=1, keepdims=True) > 0
     total = mine[...]
-    squares = sq[:, :1]
     for k in range(parts.shape[0]):
         total += parts[k].astype(F32)
-        squares += sqs[k][:, :1]
-    inv = lax.rsqrt(squares / inner + 1e-05)
+    feats = hidden.shape[1]
+    inv = lax.rsqrt(jnp.sum(total[:, feats:], axis=1, keepdims=True) / inner + 1e-05)
+    total = total[:, :feats]
     delta = lax.dot_general(
         onehot.astype(F32), inv * total, TN,
         precision=lax.Precision.HIGHEST, preferred_element_type=F32,
@@ -568,15 +600,14 @@
     ]
     for copy in outs:
         copy.start()
-    lax.fori_loop(1, seqs // 2, step, 0)
+
+    def drain(p, carry):
+        write(st, p).wait()
+        return carry
+
+    lax.fori_loop(0, seqs // 2, drain, 0)
     for copy in outs:
         copy.wait()
-
-    def drain(p, carry):
-        write(p).wait()
-        return carry
-
-    lax.fori_loop(0, seqs // 2, drain, 0)
 
 
 def shards(n, *args):
@@ -601,6 +632,7 @@
     bc_own = bc_weight.shape[1]
     heads, hp, ns = ssm_state.shape[1:]
     steps = STEPS
+    ready = READY
     in_hbm = lambda v: pltpu.with_memory_space_constraint(v, pltpu.HBM)
     active = active.reshape(1, -1)
     x_old = jnp.transpose(conv_x_state, (1, 0, 2))
@@ -608,22 +640,20 @@
     dma = pltpu.SemaphoreType.DMA
     shape = jax.ShapeDtypeStruct
     like = lambda v: pltpu.VMEM(v.shape, v.dtype)
-    x_new, bcp, ut, b_rows, dec, mine, sq, parts, sqs, held = pl.pallas_call(
-        functools.partial(front_kernel, n, steps),
+    x_new, bcp, ut, b_rows, dec, mine, parts, held = pl.pallas_call(
+        functools.partial(front_kernel, n, steps, ready),
         out_shape=(
             pltpu.VMEM((seqs, chans), BF16),
             pltpu.VMEM((seqs, bc_own), BF16),
             pltpu.VMEM((chans, 2 * seqs), BF16),
             pltpu.VMEM((seqs, ns), F32),
             pltpu.VMEM((heads, seqs, ns), F32),
-            pltpu.VMEM((seqs, feats), F32),
-            pltpu.VMEM((seqs, 128), F32),
-            pltpu.VMEM((n - 1, seqs, feats), BF16),
-            pltpu.VMEM((n - 1, seqs, 128), F32),
+            pltpu.VMEM((seqs, feats + 128), F32),
+            pltpu.VMEM((n - 1, seqs, feats + 128), BF16),
             pltpu.VMEM(ssm_state.shape, F32),
         ),
         in_specs=[HBM] * 20,
-        out_specs=(VMEM,) * 10,
+        out_specs=(VMEM,) * 8,
         scratch_shapes=[
             like(hidden),
             pltpu.VMEM((n, seqs, feats), BF16),
@@ -635,12 +665,11 @@
             pltpu.VMEM((seqs, bc_own), BF16),
             pltpu.VMEM((n, seqs, bc_own), BF16),
             pltpu.VMEM((chans, 128), F32),
-            pltpu.VMEM((n, seqs, feats), BF16),
+            pltpu.VMEM((n, seqs, feats + 128), BF16),
             like(in_gain), like(conv_x_weight), like(conv_x_bias), like(x_old),
             like(conv_bc_weight), like(conv_bc_bias), like(bc_old),
             like(dt_bias), like(log_rate), like(skip_gain), like(norm_gain), like(pool_slot), like(active),
-            dma(()), dma((15,)), dma((n,)), dma((n,)), dma((steps,)), dma((n,)),
-            dma((n,)), dma((n,)), dma((n,)), dma((n,)), dma((n,)), dma((n,)), dma((n,)), dma((n,)),
+            dma((n - 1,)), dma((n - 1,)), dma((n - 1,)),
         ],
         compiler_params=pltpu.CompilerParams(
             collective_id=0, has_side_effects=True, vmem_limit_bytes=28 * 2**20
@@ -652,14 +681,14 @@
         dt_bias, log_rate, skip_gain, norm_gain, pool_slot, active, ssm_state,
     )))
     layer_out, x_next, bc_next, state_next = pl.pallas_call(
-        functools.partial(back_kernel, chans * n),
+        functools.partial(back_kernel, chans * n, ready),
         out_shape=(
             shape(hidden.shape, BF16),
             shape(x_old.shape, BF16),
             shape(bc_old.shape, BF16),
             shape(ssm_state.shape, F32),
         ),
-        in_specs=[VMEM] * 15,
+        in_specs=[VMEM] * 13,
         out_specs=(HBM,) * 4,
         scratch_shapes=[
             like(hidden), like(x_old), like(bc_old), like(ssm_state),
@@ -668,7 +697,7 @@
         compiler_params=pltpu.CompilerParams(vmem_limit_bytes=16 * 2**20),
         name="back",
     )(
-        hidden, pool_slot, active, mine, sq, parts, sqs, x_new, x_old, bcp, bc_old, ut, b_rows, dec, held,
+        hidden, pool_slot, active, mine, parts, x_new, x_old, bcp, bc_old, ut, b_rows, dec, held,
     )
     return (
         layer_out,

time: 20.5 us -> 19.5 us (0.951)
  Pallas kernels: 19.6 us -> 18.6 us
    pallas_call x2, Pallas kernels: 19.6 us -> 18.6 us  [the longest x1 14.5 us: fast_shards(): pl.pallas_call(functools.partial(front_kernel, n, steps, ready), out_shap...]
where the time goes in v3:
time: 19.5 us; the launch traced here: 19.3 us
  Pallas kernels  18.6 us (95%)
  between operations  0.73 us (4%)
    pallas_call x1, Pallas kernels, fast_shards(): pl.pallas_call(functools.partial(front_kernel, n, steps, ready), out_shap...  14.5 us
    pallas_call x1, Pallas kernels, fast_shards(): pl.pallas_call(functools.partial(back_kernel, chans * n, ready), out_shap...  4.12 us

profile of v3, /device:TPU:0, one launch (start us, length us, event | category | flops | bytes accessed | tf_op | source)
XLA Modules:
  0.0 19.3 jit_solution(14519959108153092858)
XLA Ops:
  0.6 0.0 copy-start
  0.6 0.0 copy-start.1
  0.7 0.0 copy-start.2
  0.7 0.0 copy-start.3
  0.7 0.0 copy-start.4
  0.7 14.5 %front.1 = (bf16[16,1280]{1,0:T(8,128)(2,1)S(1)}, bf16[16,64]{1,0:T(8,128)(2,1)S(1)}, bf16[1280,32]{1,0:T(8,128)(2,1)S(1)}, f32[16,128]{1,0:T(8,128)S(1)}, f32[2...) custom-call(bf16[16,640]{1,0:T(8,128)(2,1)} %hidden.1, ...), custom_call_target="tpu_custom_call" | custom-call | tf_op jit(solution)/shard_map/front/pallas_call | solution.py:643
  15.2 0.0 copy-done
  15.2 0.0 copy-done.1
  15.2 0.0 copy-done.2
  15.2 0.0 copy-done.3
  15.2 0.0 copy-done.4
  15.2 4.1 %back.1 = (bf16[16,640]{1,0:T(8,128)(2,1)}, bf16[3,16,1280]{2,1,0:T(8,128)(2,1)}, bf16[3,16,64]{2,1,0:T(8,128)(2,1)}, f32[16,20,64,128]{3,2,1,0:T(8,128)}) custom-call(bf16[16,640]{1,0:T(8,128)(2,1)S(1)} %copy-done.1, s32[1,16]{1,0:T(1,128)S(1)} %copy-done.3, s32[1,16]{1,0:T(1,128)S(1)} %bitcast.12, f32[16,768]{1,0:T(8,128)S(1)} %get-tuple-element.16.mine, ...), custom_call_target="tpu_custom_call" | custom-call | tf_op jit(solution)/shard_map/back/pallas_call | solution.py:683
Async XLA Ops:
  0.6 14.5 %copy-start = (bf16[16,3,1280]{2,0,1:T(8,128)(2,1)S(1)}, bf16[16,3,1280]{2,0,1:T(8,128)(2,1)}, u32[]{:S(2)}) copy-start(bf16[16,3,1280]{2,0,1:T(8,128)(2,1)} %param.30) | copy-start | bytes 368644
  0.6 14.5 %copy-start.1 = (bf16[16,640]{1,0:T(8,128)(2,1)S(1)}, bf16[16,640]{1,0:T(8,128)(2,1)}, u32[]{:S(2)}) copy-start(bf16[16,640]{1,0:T(8,128)(2,1)} %hidden.1) | copy-start | bytes 61444
  0.7 14.5 %copy-start.2 = (bf16[16,3,64]{2,0,1:T(8,128)(2,1)S(1)}, bf16[16,3,64]{2,0,1:T(8,128)(2,1)}, u32[]{:S(2)}) copy-start(bf16[16,3,64]{2,0,1:T(8,128)(2,1)} %param.31) | copy-start | bytes 18436
  0.7 14.5 %copy-start.3 = (s32[1,16]{1,0:T(1,128)S(1)}, s32[1,16]{1,0:T(1,128)}, u32[]{:S(2)}) copy-start(s32[1,16]{1,0:T(1,128)} %slot.1) | copy-start | bytes 196
  0.7 14.5 %copy-start.4 = (s32[16]{0:T(128)S(1)}, s32[16]{0:T(128)}, u32[]{:S(2)}) copy-start(s32[16]{0:T(128)} %param.39) | copy-start | bytes 196

commit v4 on v3

--- a/solution.py
+++ b/solution.py
@@ -15,9 +15,10 @@
 HBM = pl.BlockSpec(memory_space=pltpu.HBM)
 NT = (((1,), (1,)), ((), ()))
 TN = (((0,), (0,)), ((), ()))
-STEPS = 4
-ROWS = 256
+STEPS = 8
+ROWS = 128
 READY = 4
+GROUPS = ((0, 1, 2, 3), (4, 5), (6,), (7,))
 
 
 def silu(v):
@@ -301,7 +302,7 @@
     dma = pltpu.SemaphoreType.DMA
     pl.run_scoped(
         functools.partial(front_body, n, steps, ready, *refs),
-        dma(()), dma((15,)), dma((n,)), dma((n,)), dma((steps,)), dma((n,)), dma((n,)), dma((n,)), dma((n,)),
+        dma(()), dma((15,)), dma((n,)), dma((n,)), dma((steps,)), dma((n,)), dma((n,)), dma((n,)), dma((n,)), dma((n,)),
     )
 
 
@@ -309,11 +310,11 @@
     n, steps, ready,
     hidden, gain_h, zw, xw, bcw_h, dtw_h, ow_h, x_taps_h, x_bias_h, x_state_h,
     bc_taps_h, bc_bias_h, bc_state_h, dt_bias_h, log_rate_h, skip_h, norm_gain_h, slot_h, active_h, state_h,
-    x_out, bcp_out, ut_out, b_out, dec_out, mine_out, parts, state_out,
+    x_out, bcp_out, ut_out, b_out, dec_out, mine_out, sq_out, parts, sqs, state_out,
     own, hid, zbuf, xbuf, bcw, dtw, owbuf, bc_send, bc_all, yt, part_send,
     gain, x_taps, x_bias, x_state, bc_taps, bc_bias, bc_state, dt_bias, log_rate, skip, norm_gain, slot, active,
-    hr, br, pr,
-    own_sem, small_sem, xsem, zsem, ssem, wsem, hs, bs, ps,
+    hr, br, pr, qr,
+    own_sem, small_sem, xsem, zsem, ssem, wsem, hs, bs, ps, qs,
 ):
     me = lax.axis_index("tp")
     seqs, feats = hidden.shape
@@ -414,7 +415,7 @@
         if k == 1:
             xc[1].wait()
             x += jnp.dot(feeds[1], xbuf[1], preferred_element_type=F32)
-            stream(stc[: steps // 2])
+            stream(stc)
             zc[1].wait()
             z += jnp.dot(feeds[1], zbuf[1], preferred_element_type=F32)
     inv = lax.rsqrt(squares / (n * feats) + 1e-05)
@@ -428,14 +429,13 @@
     bc_swaps = {k: swap(bc_send, bc_all.at[me], bs, br, k) for k in far}
     for k in far:
         bc_swaps[k].start()
-    stream(stc[steps // 2 :])
 
     for k in far[:-1]:
         xc[k].wait()
         x += jnp.dot(feeds[k], xbuf[k], preferred_element_type=F32)
         zc[k].wait()
         z += jnp.dot(feeds[k], zbuf[k], preferred_element_type=F32)
-    stream([owc[k] for k in far[:2]])
+    stream([owc[k] for k in far[:-1]])
     dt = softplus((dtp * inv).astype(BF16).astype(F32) + dt_bias[...].reshape(1, -1))
     decay = jnp.where(live, jnp.exp(-dt * jnp.exp(log_rate[...].reshape(1, -1))), 1.0)
     for h in range(heads):
@@ -467,7 +467,7 @@
 
     for k in far:
         bc_swaps[k].wait_recv()
-    stream([owc[k] for k in far[2:] + [0]])
+    stream([owc[far[-1]], owc[0]])
     both = jnp.concatenate([bc_all[j] for j in range(n)], axis=1).astype(F32)
     b_rows = both[:, :ns]
     c_rows = both[:, ns:]
@@ -476,50 +476,53 @@
     row_id = lax.broadcasted_iota(jnp.int32, (seqs, ns), 0)
     tile = ROWS if chans % ROWS == 0 else chans
     old_y = []
-    for q in range(steps):
+    for g, group in enumerate(GROUPS):
+        rows = [q * span + i for q in group for i in range(span)]
         stationary = jnp.concatenate(
-            [jnp.where(row_id == q * span + i, c_rows, 0.0).astype(BF16) for i in range(span)], axis=1
+            [jnp.where(row_id == b, c_rows, 0.0).astype(BF16) for b in rows], axis=1
         )
         stationary = jnp.concatenate(
-            [stationary, jnp.zeros((128 - seqs, span * ns), BF16)], axis=0
+            [stationary, jnp.zeros((128 - seqs, len(rows) * ns), BF16)], axis=0
         )
-        stc[q].wait()
+        for q in group:
+            stc[q].wait()
         for lo in range(0, chans, tile):
             moving = jnp.concatenate(
-                [
-                    state_out[q * span + i, lo // hp : (lo + tile) // hp].reshape(tile, ns).astype(BF16)
-                    for i in range(span)
-                ],
+                [state_out[b, lo // hp : (lo + tile) // hp].reshape(tile, ns).astype(BF16) for b in rows],
                 axis=1,
             )
             got = lax.dot_general(moving, stationary, NT, preferred_element_type=F32)
-            if q == 0:
-                yt[lo : lo + tile, :] = got
-            elif q < steps - 1:
+            if g == len(GROUPS) - 1:
+                old_y.append((yt[lo : lo + tile, :] + got).T[:seqs])
+            elif g:
                 yt[lo : lo + tile, :] += got
             else:
-                old_y.append((yt[lo : lo + tile, :] + got).T[:seqs])
+                yt[lo : lo + tile, :] = got
     old_y = jnp.concatenate(old_y, axis=1)
     y = decay_wide * old_y + u * along + skip_wide * conv
     gated = y * gate
-    sq = jnp.sum(gated * gated, axis=1, keepdims=True)
-    high = sq.astype(BF16).astype(F32)
-    mid = (sq - high).astype(BF16).astype(F32)
-    lane = lax.broadcasted_iota(jnp.int32, (seqs, 128), 1)
-    rest = jnp.where(lane == 1, mid, sq - high - mid)
-    coded = jnp.where(lane == 0, high, jnp.where(lane < 3, rest, 0.0))
-    for k in far:
-        part_send[k, :, feats:] = coded.astype(BF16)
-    mine_out[:, feats:] = coded
     scaled = (gated * norm_gain[...].reshape(1, -1)).astype(BF16)
     tails = []
-    for k in far:
-        owc[k].wait()
-        part_send[k, :, :feats] = jnp.dot(scaled, owbuf[k], preferred_element_type=F32).astype(BF16)
-        tails.append(swap(part_send.at[k], parts.at[k - 1], ps, pr, k))
-        tails[-1].start()
-    owc[0].wait()
-    mine_out[:, :feats] = jnp.dot(scaled, owbuf[0], preferred_element_type=F32)
+    started = False
+    for group in [[k] for k in far[:-1]] + [[far[-1], 0]]:
+        for k in group:
+            owc[k].wait()
+        columns = jnp.concatenate([owbuf[k] for k in group], axis=1)
+        got = jnp.dot(scaled, columns, preferred_element_type=F32)
+        for i, k in enumerate(group):
+            piece = got[:, i * feats : (i + 1) * feats]
+            if k == 0:
+                mine_out[...] = piece
+            else:
+                part_send[k] = piece.astype(BF16)
+                tails.append(swap(part_send.at[k], parts.at[k - 1], ps, pr, k))
+                tails[-1].start()
+        if not started:
+            started = True
+            sq_out[...] = jnp.broadcast_to(jnp.sum(gated * gated, axis=1, keepdims=True), sq_out.shape)
+            for k in far:
+                tails.append(swap(sq_out, sqs.at[k - 1], qs, qr, k))
+                tails[-1].start()
     for p in range(ready):
         update(p, dec_out, ut_out, b_out, state_out, state_out)
     for copies in (hid_swaps, bc_swaps):
@@ -553,7 +556,7 @@
 
 def back_kernel(
     inner, ready,
-    hidden, slot, active, mine, parts, x_new, x_state, bcp, bc_state, ut, b_rows, dec, state,
+    hidden, slot, active, mine, sq, parts, sqs, x_new, x_state, bcp, bc_state, ut, b_rows, dec, state,
     layer_h, x_next_h, bc_next_h, state_next,
     layer, x_next, bc_next, st, osem, lsem,
 ):
@@ -583,11 +586,11 @@
     )
     live = jnp.sum(jnp.where(eye, active[...], 0), axis=1, keepdims=True) > 0
     total = mine[...]
+    squares = sq[:, :1]
     for k in range(parts.shape[0]):
         total += parts[k].astype(F32)
-    feats = hidden.shape[1]
-    inv = lax.rsqrt(jnp.sum(total[:, feats:], axis=1, keepdims=True) / inner + 1e-05)
-    total = total[:, :feats]
+        squares += sqs[k][:, :1]
+    inv = lax.rsqrt(squares / inner + 1e-05)
     delta = lax.dot_general(
         onehot.astype(F32), inv * total, TN,
         precision=lax.Precision.HIGHEST, preferred_element_type=F32,
@@ -640,7 +643,7 @@
     dma = pltpu.SemaphoreType.DMA
     shape = jax.ShapeDtypeStruct
     like = lambda v: pltpu.VMEM(v.shape, v.dtype)
-    x_new, bcp, ut, b_rows, dec, mine, parts, held = pl.pallas_call(
+    x_new, bcp, ut, b_rows, dec, mine, sq, parts, sqs, held = pl.pallas_call(
         functools.partial(front_kernel, n, steps, ready),
         out_shape=(
             pltpu.VMEM((seqs, chans), BF16),
@@ -648,12 +651,14 @@
             pltpu.VMEM((chans, 2 * seqs), BF16),
             pltpu.VMEM((seqs, ns), F32),
             pltpu.VMEM((heads, seqs, ns), F32),
-            pltpu.VMEM((seqs, feats + 128), F32),
-            pltpu.VMEM((n - 1, seqs, feats + 128), BF16),
+            pltpu.VMEM((seqs, feats), F32),
+            pltpu.VMEM((seqs, 128), F32),
+            pltpu.VMEM((n - 1, seqs, feats), BF16),
+            pltpu.VMEM((n - 1, seqs, 128), F32),
             pltpu.VMEM(ssm_state.shape, F32),
         ),
         in_specs=[HBM] * 20,
-        out_specs=(VMEM,) * 8,
+        out_specs=(VMEM,) * 10,
         scratch_shapes=[
             like(hidden),
             pltpu.VMEM((n, seqs, feats), BF16),
@@ -665,11 +670,11 @@
             pltpu.VMEM((seqs, bc_own), BF16),
             pltpu.VMEM((n, seqs, bc_own), BF16),
             pltpu.VMEM((chans, 128), F32),
-            pltpu.VMEM((n, seqs, feats + 128), BF16),
+            pltpu.VMEM((n, seqs, feats), BF16),
             like(in_gain), like(conv_x_weight), like(conv_x_bias), like(x_old),
             like(conv_bc_weight), like(conv_bc_bias), like(bc_old),
             like(dt_bias), like(log_rate), like(skip_gain), like(norm_gain), like(pool_slot), like(active),
-            dma((n - 1,)), dma((n - 1,)), dma((n - 1,)),
+            dma((n - 1,)), dma((n - 1,)), dma((n - 1,)), dma((n - 1,)),
         ],
         compiler_params=pltpu.CompilerParams(
             collective_id=0, has_side_effects=True, vmem_limit_bytes=28 * 2**20
@@ -688,7 +693,7 @@
             shape(bc_old.shape, BF16),
             shape(ssm_state.shape, F32),
         ),
-        in_specs=[VMEM] * 13,
+        in_specs=[VMEM] * 15,
         out_specs=(HBM,) * 4,
         scratch_shapes=[
             like(hidden), like(x_old), like(bc_old), like(ssm_state),
@@ -697,7 +702,7 @@
         compiler_params=pltpu.CompilerParams(vmem_limit_bytes=16 * 2**20),
         name="back",
     )(
-        hidden, pool_slot, active, mine, parts, x_new, x_old, bcp, bc_old, ut, b_rows, dec, held,
+        hidden, pool_slot, active, mine, sq, parts, sqs, x_new, x_old, bcp, bc_old, ut, b_rows, dec, held,
     )
     return (
         layer_out,

time: 19.5 us -> 19.1 us (0.979)
  Pallas kernels: 18.6 us -> 18.2 us
    pallas_call x1, Pallas kernels: 14.5 us -> 14.1 us  [fast_shards(): pl.pallas_call(functools.partial(front_kernel, n, steps, ready), out_shap...]
where the time goes in v4:
time: 19.1 us; the launch traced here: 19 us
  Pallas kernels  18.2 us (95%)
  between operations  0.73 us (4%)
    pallas_call x1, Pallas kernels, fast_shards(): pl.pallas_call(functools.partial(front_kernel, n, steps, ready), out_shap...  14.1 us
    pallas_call x1, Pallas kernels, fast_shards(): pl.pallas_call(functools.partial(back_kernel, chans * n, ready), out_shap...  4.12 us

profile of v4, /device:TPU:0, one launch (start us, length us, event | category | flops | bytes accessed | tf_op | source)
XLA Modules:
  0.0 19.0 jit_solution(1586366591313623529)
XLA Ops:
  0.6 0.0 copy-start
  0.6 0.0 copy-start.1
  0.7 0.0 copy-start.2
  0.7 0.0 copy-start.3
  0.7 0.0 copy-start.4
  0.7 14.1 %front.1 = (bf16[16,1280]{1,0:T(8,128)(2,1)S(1)}, bf16[16,64]{1,0:T(8,128)(2,1)S(1)}, bf16[1280,32]{1,0:T(8,128)(2,1)S(1)}, f32[16,128]{1,0:T(8,128)S(1)}, f32[2...) custom-call(bf16[16,640]{1,0:T(8,128)(2,1)} %hidden.1, ...), custom_call_target="tpu_custom_call" | custom-call | tf_op jit(solution)/shard_map/front/pallas_call | solution.py:646
  14.8 0.0 copy-done
  14.8 0.0 copy-done.1
  14.8 0.0 copy-done.2
  14.8 0.0 copy-done.3
  14.9 0.0 copy-done.4
  14.9 4.1 %back.1 = (bf16[16,640]{1,0:T(8,128)(2,1)}, bf16[3,16,1280]{2,1,0:T(8,128)(2,1)}, bf16[3,16,64]{2,1,0:T(8,128)(2,1)}, f32[16,20,64,128]{3,2,1,0:T(8,128)}) custom-call(bf16[16,640]{1,0:T(8,128)(2,1)S(1)} %copy-done.1, s32[1,16]{1,0:T(1,128)S(1)} %copy-done.3, s32[1,16]{1,0:T(1,128)S(1)} %bitcast.12, f32[16,640]{1,0:T(8,128)S(1)} %get-tuple-element.18.mine, ...), custom_call_target="tpu_custom_call" | custom-call | tf_op jit(solution)/shard_map/back/pallas_call | solution.py:688
Async XLA Ops:
  0.6 14.2 %copy-start = (bf16[16,3,1280]{2,0,1:T(8,128)(2,1)S(1)}, bf16[16,3,1280]{2,0,1:T(8,128)(2,1)}, u32[]{:S(2)}) copy-start(bf16[16,3,1280]{2,0,1:T(8,128)(2,1)} %param.30) | copy-start | bytes 368644
  0.6 14.2 %copy-start.1 = (bf16[16,640]{1,0:T(8,128)(2,1)S(1)}, bf16[16,640]{1,0:T(8,128)(2,1)}, u32[]{:S(2)}) copy-start(bf16[16,640]{1,0:T(8,128)(2,1)} %hidden.1) | copy-start | bytes 61444
  0.7 14.2 %copy-start.2 = (bf16[16,3,64]{2,0,1:T(8,128)(2,1)S(1)}, bf16[16,3,64]{2,0,1:T(8,128)(2,1)}, u32[]{:S(2)}) copy-start(bf16[16,3,64]{2,0,1:T(8,128)(2,1)} %param.31) | copy-start | bytes 18436
  0.7 14.2 %copy-start.3 = (s32[1,16]{1,0:T(1,128)S(1)}, s32[1,16]{1,0:T(1,128)}, u32[]{:S(2)}) copy-start(s32[1,16]{1,0:T(1,128)} %slot.1) | copy-start | bytes 196
  0.7 14.2 %copy-start.4 = (s32[16]{0:T(128)S(1)}, s32[16]{0:T(128)}, u32[]{:S(2)}) copy-start(s32[16]{0:T(128)} %param.39) | copy-start | bytes 196

commit v5 on v4

--- a/solution.py
+++ b/solution.py
@@ -311,8 +311,9 @@
     hidden, gain_h, zw, xw, bcw_h, dtw_h, ow_h, x_taps_h, x_bias_h, x_state_h,
     bc_taps_h, bc_bias_h, bc_state_h, dt_bias_h, log_rate_h, skip_h, norm_gain_h, slot_h, active_h, state_h,
     x_out, bcp_out, ut_out, b_out, dec_out, mine_out, sq_out, parts, sqs, state_out,
-    own, hid, zbuf, xbuf, bcw, dtw, owbuf, bc_send, bc_all, yt, part_send,
-    gain, x_taps, x_bias, x_state, bc_taps, bc_bias, bc_state, dt_bias, log_rate, skip, norm_gain, slot, active,
+    own, x_state, bc_state, slot, active,
+    hid, zbuf, xbuf, bcw, dtw, owbuf, bc_send, bc_all, yt, part_send,
+    gain, x_taps, x_bias, bc_taps, bc_bias, dt_bias, log_rate, skip, norm_gain,
     hr, br, pr, qr,
     own_sem, small_sem, xsem, zsem, ssem, wsem, hs, bs, ps, qs,
 ):
@@ -556,7 +557,7 @@
 
 def back_kernel(
     inner, ready,
-    hidden, slot, active, mine, sq, parts, sqs, x_new, x_state, bcp, bc_state, ut, b_rows, dec, state,
+    hidden, x_state, bc_state, slot, active, mine, sq, parts, sqs, x_new, bcp, ut, b_rows, dec, state,
     layer_h, x_next_h, bc_next_h, state_next,
     layer, x_next, bc_next, st, osem, lsem,
 ):
@@ -643,7 +644,7 @@
     dma = pltpu.SemaphoreType.DMA
     shape = jax.ShapeDtypeStruct
     like = lambda v: pltpu.VMEM(v.shape, v.dtype)
-    x_new, bcp, ut, b_rows, dec, mine, sq, parts, sqs, held = pl.pallas_call(
+    x_new, bcp, ut, b_rows, dec, mine, sq, parts, sqs, held, *kept = pl.pallas_call(
         functools.partial(front_kernel, n, steps, ready),
         out_shape=(
             pltpu.VMEM((seqs, chans), BF16),
@@ -656,11 +657,11 @@
             pltpu.VMEM((n - 1, seqs, feats), BF16),
             pltpu.VMEM((n - 1, seqs, 128), F32),
             pltpu.VMEM(ssm_state.shape, F32),
+            like(hidden), like(x_old), like(bc_old), like(pool_slot), like(active),
         ),
         in_specs=[HBM] * 20,
-        out_specs=(VMEM,) * 10,
+        out_specs=(VMEM,) * 15,
         scratch_shapes=[
-            like(hidden),
             pltpu.VMEM((n, seqs, feats), BF16),
             pltpu.VMEM((n, feats, chans), BF16),
             pltpu.VMEM((n, feats, chans), BF16),
@@ -671,9 +672,8 @@
             pltpu.VMEM((n, seqs, bc_own), BF16),
             pltpu.VMEM((chans, 128), F32),
             pltpu.VMEM((n, seqs, feats), BF16),
-            like(in_gain), like(conv_x_weight), like(conv_x_bias), like(x_old),
-            like(conv_bc_weight), like(conv_bc_bias), like(bc_old),
-            like(dt_bias), like(log_rate), like(skip_gain), like(norm_gain), like(pool_slot), like(active),
+            like(in_gain), like(conv_x_weight), like(conv_x_bias), like(conv_bc_weight), like(conv_bc_bias),
+            like(dt_bias), like(log_rate), like(skip_gain), like(norm_gain),
             dma((n - 1,)), dma((n - 1,)), dma((n - 1,)), dma((n - 1,)),
         ],
         compiler_params=pltpu.CompilerParams(
@@ -702,7 +702,7 @@
         compiler_params=pltpu.CompilerParams(vmem_limit_bytes=16 * 2**20),
         name="back",
     )(
-        hidden, pool_slot, active, mine, sq, parts, sqs, x_new, x_old, bcp, bc_old, ut, b_rows, dec, held,
+        *kept, mine, sq, parts, sqs, x_new, bcp, ut, b_rows, dec, held,
     )
     return (
         layer_out,

time: 19.1 us -> 19.1 us (level)
  no operation moved by 1% of the time
where the time goes in v5:
time: 19.1 us; the launch traced here: 18.9 us
  Pallas kernels  18.3 us (96%)
  between operations  0.65 us (3%)
    pallas_call x1, Pallas kernels, fast_shards(): pl.pallas_call(functools.partial(front_kernel, n, steps, ready), out_shap...  14.1 us
    pallas_call x1, Pallas kernels, fast_shards(): pl.pallas_call(functools.partial(back_kernel, chans * n, ready), out_shap...  4.12 us

profile of v5, /device:TPU:0, one launch (start us, length us, event | category | flops | bytes accessed | tf_op | source)
XLA Modules:
  0.0 18.9 jit_solution(115760008676966551)
XLA Ops:
  0.6 14.1 %front.1 = (bf16[16,1280]{1,0:T(8,128)(2,1)S(1)}, bf16[16,64]{1,0:T(8,128)(2,1)S(1)}, bf16[1280,32]{1,0:T(8,128)(2,1)S(1)}, f32[16,128]{1,0:T(8,128)S(1)}, f32[2...) custom-call(bf16[16,640]{1,0:T(8,128)(2,1)} %refs_0_.1, ...), custom_call_target="tpu_custom_call" | custom-call | tf_op jit(solution)/shard_map/front/pallas_call | solution.py:647
  14.8 4.1 %back.1 = (bf16[16,640]{1,0:T(8,128)(2,1)}, bf16[3,16,1280]{2,1,0:T(8,128)(2,1)}, bf16[3,16,64]{2,1,0:T(8,128)(2,1)}, f32[16,20,64,128]{3,2,1,0:T(8,128)}) custom-call(bf16[16,640]{1,0:T(8,128)(2,1)S(1)} %get-tuple-element.23.hidden, bf16[3,16,1280]{2,1,0:T(8,128)(2,1)S(1)} %get-tuple-element.24.x_state, bf16[3,16,64]{2,1,0:T(8,128)(2,1)S(1)} %get-tuple-element.25.bc_state, ...), custom_call_target="tpu_custom_call" | custom-call | tf_op jit(solution)/shard_map/back/pallas_call | solution.py:688

commit v6 on v5

--- a/solution.py
+++ b/solution.py
@@ -17,7 +17,7 @@
 TN = (((0,), (0,)), ((), ()))
 STEPS = 8
 ROWS = 128
-READY = 4
+READY = 3
 GROUPS = ((0, 1, 2, 3), (4, 5), (6,), (7,))
 
 
@@ -356,6 +356,7 @@
 
     for k in range(n):
         stream([xc[k], zc[k]])
+    stream(stc[:2])
 
     barrier = pltpu.get_barrier_semaphore()
     for k in range(1, n):
@@ -400,6 +401,7 @@
     squares = squared(0)
     xc[0].wait()
     x = jnp.dot(feed, xbuf[0], preferred_element_type=F32)
+    stream(stc[2:])
     zc[0].wait()
     z = jnp.dot(feed, zbuf[0], preferred_element_type=F32)
     for copy in smalls[-2:]:
@@ -416,7 +418,6 @@
         if k == 1:
             xc[1].wait()
             x += jnp.dot(feeds[1], xbuf[1], preferred_element_type=F32)
-            stream(stc)
             zc[1].wait()
             z += jnp.dot(feeds[1], zbuf[1], preferred_element_type=F32)
     inv = lax.rsqrt(squares / (n * feats) + 1e-05)

time: 19.1 us -> 19.1 us (level)
  no operation moved by 1% of the time
where the time goes in v6:
time: 19.1 us; the launch traced here: 18.9 us
  Pallas kernels  18.3 us (96%)
  between operations  0.65 us (3%)
    pallas_call x1, Pallas kernels, fast_shards(): pl.pallas_call(functools.partial(front_kernel, n, steps, ready), out_shap...  14.1 us
    pallas_call x1, Pallas kernels, fast_shards(): pl.pallas_call(functools.partial(back_kernel, chans * n, ready), out_shap...  4.12 us

profile of v6, /device:TPU:0, one launch (start us, length us, event | category | flops | bytes accessed | tf_op | source)
XLA Modules:
  0.0 18.9 jit_solution(7092712766787234106)
XLA Ops:
  0.6 14.1 %front.1 = (bf16[16,1280]{1,0:T(8,128)(2,1)S(1)}, bf16[16,64]{1,0:T(8,128)(2,1)S(1)}, bf16[1280,32]{1,0:T(8,128)(2,1)S(1)}, f32[16,128]{1,0:T(8,128)S(1)}, f32[2...) custom-call(bf16[16,640]{1,0:T(8,128)(2,1)} %refs_0_.1, ...), custom_call_target="tpu_custom_call" | custom-call | tf_op jit(solution)/shard_map/front/pallas_call | solution.py:648
  14.8 4.1 %back.1 = (bf16[16,640]{1,0:T(8,128)(2,1)}, bf16[3,16,1280]{2,1,0:T(8,128)(2,1)}, bf16[3,16,64]{2,1,0:T(8,128)(2,1)}, f32[16,20,64,128]{3,2,1,0:T(8,128)}) custom-call(bf16[16,640]{1,0:T(8,128)(2,1)S(1)} %get-tuple-element.23.hidden, bf16[3,16,1280]{2,1,0:T(8,128)(2,1)S(1)} %get-tuple-element.24.x_state, bf16[3,16,64]{2,1,0:T(8,128)(2,1)S(1)} %get-tuple-element.25.bc_state, ...), custom_call_target="tpu_custom_call" | custom-call | tf_op jit(solution)/shard_map/back/pallas_call | solution.py:689
